TPU v7x, 256 devices: a whole 4x4x8 slice. The times are simulated.
256 devices in a mesh: dp: 32 (over y, x, core), feat: 8 (over z).
Axes of the slice: x: 4, y: 4, z: 8, core: 2. Of those that a mesh axis runs over, the one named last changes fastest.
Arguments:
- hidden_states: bfloat16 [512, 256, 1152], P(('dp', 'feat')), may hold values from -6 to 6
- teacher: bfloat16 [512, 256, 1024], P('dp', None, 'feat'), may hold values from -6 to 6
- proj_in: bfloat16 [2048, 1152], replicated, may hold values from -0.1875 to 0.1875
- bias_in: float32 [2048], replicated, may hold values from -3 to 3
- proj_out: bfloat16 [2048, 1024], replicated, may hold values from -0.125 to 0.125
- bias_out: float32 [1024], replicated, may hold values from -3 to 3
Outputs:
- grad_proj_in: float32 [2048, 1152], P(('dp', 'feat'))
- grad_bias_in: float32 [2048], P(('dp', 'feat'))
- grad_proj_out: float32 [2048, 1024], P(('dp', 'feat'))
- grad_bias_out: float32 [1024], replicated
- grad_hidden: bfloat16 [512, 256, 1152], P(('dp', 'feat'))
- loss: float32 [], replicated
All inputs are finite; a program needn't handle non-finite values.
Results may differ from a plain program's by a relative error of at most 0.0095.
The roundings to bfloat16 on the way count: a program that leaves them out, or rounds other values in their place, can miss the bound.
Values may be sent and summed in bfloat16 or wider, within the bound.
No kernel may reach another device: no remote copies, remote signals or barrier semaphores. Data moves between devices by JAX's collectives and lax.ppermute only.
A program may use at most 128 MiB of HBM per device.

v0:
```python
import functools

import jax
import jax.numpy as jnp
from jax import lax
from jax.sharding import Mesh
from jax.sharding import PartitionSpec as P

DP = ("dp_0", "dp_1", "dp_2")
DP_FEAT = ("dp_0", "dp_1", "dp_2", "feat")


epsilon = 1e-06


def by_axis(x, axes):
    return functools.reduce(lax.psum, axes, x)


def on_device(hidden_states, teacher, proj_in, bias_in, proj_out, bias_out):
    samples, seq, width = hidden_states.shape
    hidden_units = proj_in.shape[0]
    channels = proj_out.shape[1]
    rows = hidden_states.reshape(samples * seq, width)
    devices = lax.axis_size(DP) * lax.axis_size("feat")
    share = hidden_units // devices
    scale = 1.0 / float(samples * seq * devices)
    pre = (
        lax.dot_general(rows, proj_in, (((1,), (1,)), ((), ())), preferred_element_type=jnp.float32)
        + bias_in
    )
    act = jax.nn.silu(pre).astype(jnp.bfloat16)
    out = jnp.dot(act, proj_out, preferred_element_type=jnp.float32) + bias_out
    target = (
        lax.all_to_all(teacher, "feat", split_axis=0, concat_axis=2, tiled=True)
        .reshape(samples * seq, channels)
        .astype(jnp.float32)
    )
    zz = jnp.sum(out * out, axis=1)
    yy = jnp.sum(target * target, axis=1)
    zy = jnp.sum(out * target, axis=1)
    norm_z = jnp.sqrt(zz + epsilon)
    norm_y = jnp.sqrt(yy + epsilon)
    cosine = zy / (norm_z * norm_y)
    cot = (
        -(target / (norm_z * norm_y)[:, None] - (cosine / (norm_z * norm_z))[:, None] * out)
    ).astype(jnp.bfloat16)
    loss_part = jnp.sum(cosine)
    bias_out_part = jnp.sum(cot.astype(jnp.float32), axis=0)
    back = lax.dot_general(
        cot, proj_out, (((1,), (1,)), ((), ())), preferred_element_type=jnp.float32
    )
    sig = jax.nn.sigmoid(pre)
    dpre = (back * sig * (1.0 + pre * (1.0 - sig))).astype(jnp.bfloat16)
    grad_hidden = (
        jnp.dot(dpre, proj_in, preferred_element_type=jnp.float32)
        .astype(jnp.bfloat16)
        .reshape(samples, seq, width)
    )
    bias_in_part = jnp.sum(dpre.astype(jnp.float32), axis=0)
    first = lax.dot_general(
        dpre, rows, (((0,), (0,)), ((), ())), preferred_element_type=jnp.float32
    )
    last = lax.dot_general(act, cot, (((0,), (0,)), ((), ())), preferred_element_type=jnp.float32)
    joint = lax.psum_scatter(
        jnp.concatenate([first, last], axis=1), DP_FEAT, scatter_dimension=0, tiled=True
    )
    grad_first = joint[:, :width]
    grad_last = joint[:, width:]
    bias_in_sum, bias_out_sum, loss_sum = (
        by_axis(bias_in_part, DP_FEAT),
        by_axis(bias_out_part, DP_FEAT),
        by_axis(loss_part, DP_FEAT),
    )
    owner = lax.axis_index(DP) * lax.axis_size("feat") + lax.axis_index("feat")
    grad_bias_first = lax.dynamic_slice_in_dim(bias_in_sum, owner * share, share, 0)
    return (
        grad_first * scale,
        grad_bias_first * scale,
        grad_last * scale,
        bias_out_sum * scale,
        grad_hidden,
        -loss_sum * scale,
    )


def solution(mesh):
    finer = Mesh(
        mesh.devices.reshape(4, 4, 2, mesh.shape["feat"]), ("dp_0", "dp_1", "dp_2", "feat")
    )
    return jax.shard_map(
        on_device,
        mesh=finer,
        in_specs=(P(DP_FEAT, None, None), P(DP, None, "feat"), P(), P(), P(), P()),
        out_specs=(
            P(DP_FEAT, None),
            P(DP_FEAT),
            P(DP_FEAT, None),
            P(),
            P(DP_FEAT, None, None),
            P(),
        ),
        check_vma=False,
    )
```

profile of v0, /device:TPU:6, one launch (start us, length us, event | category | flops | bytes accessed | tf_op | source)
XLA Modules:
  0.0 378.6 jit_solution(17967677392415455112)
XLA Ops:
  7.2 8.6 %all-to-all-start = ((bf16[16,256,128]{2,1,0:T(8,128)(2,1)}), bf16[16,256,128]{2,1,0:T(8,128)(2,1)S(1)}, u32[]{:S(2)}, u32[]{:S(2)}) async-start(bf16[16,256,128]{2,1,0:T(8,128)(2,1)} %param.7), calls=%async_computation | async-start | bytes 2097152 | tf_op jit(solution)/shard_map/all_to_all | solution.py:35
  15.8 6.8 %fusion.9 = f32[512,2048]{1,0:T(8,128)} fusion(bf16[512,1152]{1,0:T(8,128)(2,1)S(1)} %bitcast.34, bf16[2048,1152]{1,0:T(8,128)(2,1)} %param.8), kind=kOutput, calls=%fused_computation.26 | convolution fusion | flops 2415919104 | bytes 10092544 | tf_op jit(solution)/shard_map/dot_general | solution.py:29
  22.6 21.9 %all-to-all-done = bf16[16,256,128]{2,1,0:T(8,128)(2,1)S(1)} async-done(((bf16[16,256,128]{2,1,0:T(8,128)(2,1)}), bf16[16,256,128]{2,1,0:T(8,128)(2,1)S(1)}, u32[]{:S(2)}, u32[]{:S(2)}) %all-to-all-start) | async-done | bytes 1048608 | tf_op jit(solution)/shard_map/all_to_all | solution.py:35
  44.5 0.6 multiply_reduce_fusion
  45.2 0.6 copy.21
  45.9 6.4 %multiply_reduce_fusion.1 = (f32[512]{0:T(512)S(1)}, f32[512]{0:T(512)S(1)}, f32[512,1024]{1,0:T(8,128)S(1)}) fusion(f32[1024]{0:T(1024)S(1)} %copy-done.2, f32[64,8,8,128]{3,2,1,0:T(8,128)S(1)} %bitcast.37, bf16[2048,1024]{1,0:T(8,128)(2,1)} %param.10, f32[512,2048]{1,0:T(8,128)} %fusion.9, f32[2048]{0:T(1024)S(1)} %copy-done.4), kind=kOutput, calls=%fused_computation.14 | convolution fusion | flops 2156395520 | bytes 12599296 | tf_op jit(solution)/shard_map/dot_general | solution.py:33
  52.3 0.6 divide_reduce_fusion
  52.9 0.7 convert_reduce_fusion.1
  53.6 0.9 copy-done.3
  54.5 3.3 convert_reduce_fusion
  57.8 2.6 fusion.5
  60.4 3.0 fusion.10
  63.4 6.5 %pad_maximum_fusion = f32[2048,2176]{0,1:T(8,128)} fusion(f32[2048,1024]{0,1:T(8,128)S(1)} %fusion.5, f32[2048,1152]{0,1:T(8,128)S(1)} %fusion.10), kind=kLoop, calls=%fused_computation | loop fusion | flops 4456448 | bytes 35651584 | tf_op jit(solution)/shard_map/concatenate | solution.py:66
  69.9 18.5 %all-reduce.3 = (f32[2048]{0:T(1024)S(1)}, f32[1024]{0:T(1024)S(1)}, f32[]{:T(128)}) all-reduce(f32[2048]{0:T(1024)S(1)} %get-tuple-element.49, f32[1024]{0:T(1024)S(1)} %get-tuple-element.46, f32[]{:T(128)} %get-tuple-element.44), channel_id=1, replica_groups=mesh['dp_0'=4,'dp_1'=4,'dp_2'=2,'feat'=8] {'dp_0'}, use_global_device_ids=true, to_apply=%region_6.7 | all-reduce | flops 3073 | bytes 24584 | tf_op jit(solution)/shard_map/psum | solution.py:17
  88.4 14.5 %all-reduce.2 = (f32[2048]{0:T(1024)S(1)}, f32[1024]{0:T(1024)S(1)}, f32[]{:T(128)}) all-reduce(f32[2048]{0:T(1024)S(1)} %get-tuple-element.38, f32[1024]{0:T(1024)S(1)} %get-tuple-element.39, f32[]{:T(128)} %get-tuple-element.40), channel_id=1, replica_groups=mesh['dp_0'=4,'dp_1'=4,'dp_2'=2,'feat'=8] {'dp_1'}, use_global_device_ids=true, to_apply=%region_7.8 | all-reduce | flops 3073 | bytes 24584 | tf_op jit(solution)/shard_map/psum | solution.py:17
  102.9 4.4 %all-reduce.4 = (f32[2048]{0:T(1024)S(1)}, f32[1024]{0:T(1024)S(1)}, f32[]{:T(128)}) all-reduce(f32[2048]{0:T(1024)S(1)} %get-tuple-element.35, f32[1024]{0:T(1024)S(1)} %get-tuple-element.36, f32[]{:T(128)} %get-tuple-element.37), channel_id=1, replica_groups=mesh['dp_0'=4,'dp_1'=4,'dp_2'=2,'feat'=8] {'dp_2'}, use_global_device_ids=true, to_apply=%region_8.9 | all-reduce | flops 3073 | bytes 24584 | tf_op jit(solution)/shard_map/psum | solution.py:17
  107.3 27.9 %all-reduce.1 = (f32[2048]{0:T(1024)S(1)}, f32[1024]{0:T(1024)S(1)}, f32[]{:T(128)}) all-reduce(f32[2048]{0:T(1024)S(1)} %get-tuple-element.41, f32[1024]{0:T(1024)S(1)} %get-tuple-element.42, f32[]{:T(128)} %get-tuple-element.43), channel_id=1, replica_groups=mesh['dp_0'=4,'dp_1'=4,'dp_2'=2,'feat'=8] {'feat'}, use_global_device_ids=true, to_apply=%region_9.10 | all-reduce | flops 3073 | bytes 24584 | tf_op jit(solution)/shard_map/psum | solution.py:17
  136.5 0.6 broadcast_multiply_fusion
  137.1 6.6 %convolution_convert_fusion = bf16[512,1152]{1,0:T(8,128)(2,1)} fusion(bf16[512,2048]{1,0:T(8,128)(2,1)S(1)} %copy-done.6, bf16[2048,1152]{1,0:T(8,128)(2,1)} %param.8), kind=kOutput, calls=%fused_computation.5 | convolution fusion | flops 2416508928 | bytes 7995392 | tf_op jit(solution)/shard_map/dot_general | solution.py:56
  143.7 222.8 %all-reduce.7.cloned.1.call-done = f32[2048,2176]{0,1:T(8,128)} async-done(((f32[2048,2176]{0,1:T(8,128)}), f32[2048,2176]{0,1:T(8,128)}) %all-reduce.7.cloned.1.call-update) | async-done | bytes 17825808
  366.5 1.3 dynamic-slice_multiply_fusion
  367.8 0.8 copy.23
  368.6 1.2 dynamic-slice_multiply_fusion.1
  369.9 0.8 copy.24
  (23 shorter events, 0.7 us)
Async XLA Ops:
  7.2 8.7 %copy-start = (bf16[2,256,1152]{2,1,0:T(8,128)(2,1)S(1)}, bf16[2,256,1152]{2,1,0:T(8,128)(2,1)}, u32[]{:S(2)}) copy-start(bf16[2,256,1152]{2,1,0:T(8,128)(2,1)} %param.6) | copy-start | bytes 3538948
  7.2 37.3 %all-to-all-start = ((bf16[16,256,128]{2,1,0:T(8,128)(2,1)}), bf16[16,256,128]{2,1,0:T(8,128)(2,1)S(1)}, u32[]{:S(2)}, u32[]{:S(2)}) async-start(bf16[16,256,128]{2,1,0:T(8,128)(2,1)} %param.7), calls=%async_computation | async-start | bytes 2097152 | tf_op jit(solution)/shard_map/all_to_all | solution.py:35
  15.8 350.7 %all-reduce.7.cloned.1.call-start = ((), (), s32[]{:S(2)}) async-start(), calls=%async_computation.1 | async-start | bytes 35651584
  22.6 23.2 %copy-start.2 = (f32[1024]{0:T(1024)S(1)}, f32[1024]{0:T(1024)}, u32[]{:S(2)}) copy-start(f32[1024]{0:T(1024)} %param.11) | copy-start | bytes 12292
  22.6 23.2 %copy-start.4 = (f32[2048]{0:T(1024)S(1)}, f32[2048]{0:T(1024)}, u32[]{:S(2)}) copy-start(f32[2048]{0:T(1024)} %param.9) | copy-start | bytes 24580
  45.8 7.8 %copy-start.7 = (f32[512,2048]{1,0:T(8,128)S(1)}, f32[512,2048]{1,0:T(8,128)}, u32[]{:S(2)}) copy-start(f32[512,2048]{1,0:T(8,128)} %fusion.9) | copy-start | bytes 12582916
  52.3 2.2 copy-start.3
  57.8 2.6 copy-start.5
  69.9 67.2 %copy-start.6 = (bf16[512,2048]{1,0:T(8,128)(2,1)S(1)}, bf16[512,2048]{1,0:T(8,128)(2,1)}, u32[]{:S(2)}) copy-start(bf16[512,2048]{1,0:T(8,128)(2,1)} %copy-done.5) | copy-start | bytes 6291460
  137.1 233.6 %copy-start.1 = (bf16[2,256,1152]{2,1,0:T(8,128)(2,1)S(1)}, bf16[2,256,1152]{2,1,0:T(8,128)(2,1)}, u32[]{:S(2)}) copy-start(bf16[2,256,1152]{2,1,0:T(8,128)(2,1)} %param.6) | copy-start | bytes 3538948
Sparse Core Ops, SparseCore 0:
  70.0 296.4 all-reduce.6
where the time goes:
time: 379 us
  waiting for transfers between devices  245 us (65%)
  blocking collectives  65.3 us (17%)
  matrix products  28.7 us (8%)
  between operations  16 us (4%)
  other arithmetic  12.2 us (3%)
  starting transfers between devices  8.65 us (2%)
    unnamed x2, waiting for transfers between devices  223 us
    psum x4, blocking collectives, by_axis(): return functools.reduce(lax.psum, axes, x)  65.3 us
    all_to_all x1, waiting for transfers between devices, on_device(): lax.all_to_all(teacher, 'feat', split_axis=0, concat_axis=2, tiled=True)  21.9 us
    all_to_all x1, starting transfers between devices, on_device(): lax.all_to_all(teacher, 'feat', split_axis=0, concat_axis=2, tiled=True)  8.61 us
  transfers between devices with their start and end apart: 2, of which 2 were waited for; matrix products, arithmetic and copies ran while one was open for 4% of the time, Pallas kernels for 0%

commit v1 on v0

v1 whole, which is shorter than its diff:
```python
import functools

import jax
import jax.numpy as jnp
from jax import lax
from jax.experimental import pallas as pl
from jax.experimental.pallas import tpu as pltpu
from jax.sharding import Mesh
from jax.sharding import PartitionSpec as P


Y, X, C, Z = "dp_0", "dp_1", "dp_2", "feat"
DP = (Y, X, C)
DP_FEAT = (Y, X, C, Z)

epsilon = 1e-06
f32, bf16 = jnp.float32, jnp.bfloat16
RING = 4
SHIFTS = (1, 3, 2)
ROWS = 8
MIB = 1 << 20

VMEM = pl.BlockSpec(memory_space=pltpu.VMEM)
HBM = pl.BlockSpec(memory_space=pltpu.HBM)


def shift(x, axis, k):
    n = lax.axis_size(axis)
    return lax.ppermute(x, axis, [(i, (i + k) % n) for i in range(n)])


def nt(a, b):
    return lax.dot_general(a, b, (((1,), (1,)), ((), ())), preferred_element_type=f32)


def nn(a, b):
    return jnp.dot(a, b, preferred_element_type=f32)


def high_low(v):
    high = v.astype(bf16)
    return high, (v - high.astype(f32)).astype(bf16)


def total(own, got):
    at1, at3, at2 = got
    return (own + at2) + (at1 + at3)


def call(body, ins, outs, scratch=(), flops=0, limit=16):
    return pl.pallas_call(
        body,
        out_shape=[jax.ShapeDtypeStruct(s, d) for s, d in outs],
        in_specs=ins,
        out_specs=[VMEM] * len(outs),
        scratch_shapes=list(scratch),
        compiler_params=pltpu.CompilerParams(vmem_limit_bytes=limit * MIB),
        cost_estimate=pl.CostEstimate(flops=flops, bytes_accessed=4 * MIB, transcendentals=0),
    )


def gather(w_ref, to_ref, sems, core):
    y, x = lax.axis_index(Y), lax.axis_index(X)
    block = w_ref.shape[3]
    copies = []
    for kx in range(RING):
        for ky in range(RING):
            at = kx * RING + ky
            copies.append(
                pltpu.make_async_copy(
                    w_ref.at[lax.rem(y + ky, RING), lax.rem(x + kx, RING), core],
                    to_ref.at[pl.ds(at * block, block)],
                    sems.at[at],
                )
            )
    for copy in copies:
        copy.start()
    return copies


def identity(n):
    row = lax.broadcasted_iota(jnp.int32, (n, n), 0)
    return jnp.where(row == lax.broadcasted_iota(jnp.int32, (n, n), 1), 1.0, 0.0).astype(bf16)


def turn(ref, to):
    eye = identity(ref.shape[1])

    @pl.loop(0, ref.shape[0] // 256)
    def _(i):
        at = pl.ds(pl.multiple_of(i * 256, 256), 256)
        to[:, at] = nt(eye, ref[at, :]).astype(bf16)


def first_kernel(
    rows, rows_p, w_in, w_out, bias, act_t, act_pt, slope, slope_p, act, act_p, in_mine, in_other,
    out_mine, out_other, col, s0, s1, s2, s3,
):
    y, x, c = lax.axis_index(Y), lax.axis_index(X), lax.axis_index(C)
    now = gather(w_in, in_mine, s0, c)
    later = gather(w_out, out_mine, s1, c) + gather(w_out, out_other, s2, 1 - c)
    later += gather(w_in, in_other, s3, 1 - c)
    block = w_in.shape[3]
    for kx in range(RING):
        for ky in range(RING):
            of = (lax.rem(y + ky, RING) * RING + lax.rem(x + kx, RING)) * 2 + c
            col[pl.ds((kx * RING + ky) * block, block), :] = bias[
                pl.ds(pl.multiple_of(of * block, block), block), :
            ]
    for copy in now:
        copy.wait()

    for r, a, s in ((rows, act_t, slope), (rows_p, act_pt, slope_p)):

        @pl.loop(0, r.shape[0] // 256)
        def _(i):
            at = pl.ds(pl.multiple_of(i * 256, 256), 256)
            pre = nt(in_mine[...], r[at, :]) + col[...]
            sig = jax.nn.sigmoid(pre)
            a[:, at] = (pre * sig).astype(bf16)
            s[:, at] = sig * (1.0 + pre * (1.0 - sig))

    turn(act_pt, act_p)
    turn(act_t, act)
    for copy in later:
        copy.wait()


def out_kernel(act, w, bias, out):
    @pl.loop(0, w.shape[1] // 256)
    def _(i):
        at = pl.ds(pl.multiple_of(i * 256, 256), 256)
        out[:, at] = nn(act[...], w[:, at]) + bias[:, at]


def out_more_kernel(act, w, before, out):
    @pl.loop(0, w.shape[1] // 256)
    def _(i):
        at = pl.ds(pl.multiple_of(i * 256, 256), 256)
        out[:, at] = before[:, at] + nn(act[...], w[:, at])


def cot_kernel(out, *refs):
    pieces, (cot, total_ref) = refs[:-2], refs[-2:]
    z = lax.axis_index(Z)
    n = len(pieces)
    tokens = out.shape[0]
    lanes = pieces[0].shape[1]
    total_ref[...] = jnp.zeros_like(total_ref)
    step = 64

    def of(k):
        return pl.ds(pl.multiple_of(lax.rem(z - k + n, n) * lanes, lanes), lanes)

    @pl.loop(0, tokens // step)
    def _(i):
        at = pl.ds(pl.multiple_of(i * step, step), step)
        zz = yy = zy = jnp.zeros((step, lanes), f32)
        for k, piece in enumerate(pieces):
            o, t = out[at, of(k)], piece[at, :].astype(f32)
            zz, yy, zy = zz + o * o, yy + t * t, zy + o * t
        zz, yy, zy = (jnp.sum(v, axis=1, keepdims=True) for v in (zz, yy, zy))
        norm_z = jnp.sqrt(zz + epsilon)
        norms = norm_z * jnp.sqrt(yy + epsilon)
        cosine = zy / norms
        total_ref[...] += jnp.sum(cosine)
        by_target = 1.0 / norms
        by_out = cosine / (norm_z * norm_z)
        for k, piece in enumerate(pieces):
            o, t = out[at, of(k)], piece[at, :].astype(f32)
            cot[at, of(k)] = (by_out * o - t * by_target).astype(bf16)

    high, low = high_low(jnp.broadcast_to(total_ref[0:1, 0:1], (ROWS, cot.shape[1])))
    row = lax.broadcasted_iota(jnp.int32, high.shape, 0)
    cot[pl.ds(tokens, ROWS), :] = jnp.where(
        row == 0, high.astype(f32), jnp.where(row == 1, low.astype(f32), 0.0)
    ).astype(bf16)


def back_kernel(cot, w_mine, slope, dpre):
    @pl.loop(0, slope.shape[1] // 256)
    def _(i):
        at = pl.ds(pl.multiple_of(i * 256, 256), 256)
        dpre[:, at] = (nt(w_mine[...], cot[at, :]) * slope[:, at]).astype(bf16)


def small_rows(value, width):
    high, low = high_low(value)
    pad = width - 2 * value.shape[1]
    rest = [jnp.zeros((ROWS, pad), bf16)] if pad else []
    return jnp.concatenate([high, low] + rest, axis=1)


def small_value(rows, n):
    rows = rows.astype(f32)
    return rows[:, :n] + rows[:, n : 2 * n]


def grad_in_kernel(cot_p, w_mine, slope_p, dpre, rows, rows_p, m_a, m_b, m_c, own, own_bias, dpre_p):
    back_kernel(cot_p, w_mine, slope_p, dpre_p)
    block = dpre.shape[0] // (RING * RING)
    width = rows.shape[1]
    ones = jnp.ones((ROWS, rows.shape[0]), bf16)
    bias = nt(ones, dpre[...]) + nt(ones, dpre_p[...])

    turns = ((SHIFTS[0], m_a), (SHIFTS[1], m_b), (SHIFTS[2], m_c), (0, own))

    def columns(at):
        value = nn(dpre[...], rows[:, at]) + nn(dpre_p[...], rows_p[:, at])
        for k, to in turns:
            for kx in range(RING):
                part = value[(kx * RING + k) * block : (kx * RING + k + 1) * block]
                to[kx * block : (kx + 1) * block, at] = part.astype(to.dtype)

    whole = width // 256

    @pl.loop(0, whole)
    def _(j):
        columns(pl.ds(pl.multiple_of(j * 256, 256), 256))

    if whole * 256 < width:
        columns(slice(whole * 256, width))

    for k, to in turns:
        row = lax.broadcasted_iota(jnp.int32, (ROWS, 128), 0)
        small = jnp.zeros((ROWS, 128), f32)
        for kx in range(RING):
            at = (kx * RING + k) * block
            lane = at // 128 * 128
            part = bias[:, lane : lane + 128]
            if at != lane:
                part = jnp.concatenate([part[:, block:], part[:, :block]], axis=1)
            small = jnp.where(row == kx, part, small)
        if k:
            to[RING * block :, :] = small_rows(small, width)
        else:
            own_bias[...] = small


def grad_out_kernel(act, act_p, cot, cot_p, m_a, m_b, m_c, own, own_small):
    tokens = act.shape[1]
    step = 256

    @pl.loop(0, cot.shape[1] // step)
    def _(j):
        at = pl.ds(pl.multiple_of(j * step, step), step)
        value = nn(act[...], cot[0:tokens, at]) + nn(act_p[...], cot_p[0:tokens, at])
        for k, to in zip((*SHIFTS, 0), (m_a, m_b, m_c, own)):
            to[0:step, at] = value[k * step : (k + 1) * step].astype(to.dtype)

    def sums(ref):
        return jnp.sum(ref[0:tokens, :].astype(f32), axis=0, keepdims=True)

    def cosines(ref):
        tail = ref[tokens : tokens + ROWS, 0:128].astype(f32)
        return tail[0:1] + tail[1:2]

    bias = sums(cot) + sums(cot_p)
    loss = cosines(cot) + cosines(cot_p)
    row = lax.broadcasted_iota(jnp.int32, (ROWS, 128), 0)
    small = jnp.zeros((ROWS, 128), f32)
    for r in range(ROWS):
        small = jnp.where(row == r, bias[:, r * 128 : (r + 1) * 128], small)
    small = jnp.concatenate([small, jnp.broadcast_to(loss, (ROWS, 128))], axis=1)
    packed = small_rows(small, cot.shape[1])
    for to in (m_a, m_b, m_c):
        to[step:, :] = packed
    own_small[...] = small_value(packed, 256)


def middle_kernel(by_row, own, own_small, g_a, g_b, g_c, m_a, m_b, m_c, kept, kept_small):
    height = own.shape[0]
    block = height // RING
    width = own.shape[1]
    n = own_small.shape[1]
    got = (g_a, g_b, g_c)
    small = total(own_small[...], [small_value(g[height:, 0 : 2 * n], n) for g in got])
    packed = small_rows(small, width)
    for k, to in zip((*SHIFTS, 0), (m_a, m_b, m_c, kept)):
        at = pl.ds(k * block, block)
        value = total(own[at, :], [g[at, :].astype(f32) for g in got])
        to[0:block, :] = value.astype(to.dtype)
        if by_row:
            part = jnp.broadcast_to(small[k : k + 1], small.shape)
            if k:
                to[block:, :] = small_rows(part, width)
            else:
                kept_small[...] = part
        elif k:
            to[block:, :] = packed
        else:
            kept_small[...] = small_value(packed, n)


def joint_kernel(out_own, out_small, o2, o1, o3, in_own, in_small, i2, i1, i3, joint):
    block = out_own.shape[0]
    at = 0
    for own, got in ((out_own, (o2, o1, o3)), (in_own, (i2, i1, i3))):
        value = total(own[...], [g[0:block, :].astype(f32) for g in got]).astype(bf16)
        joint[:, :, at : at + own.shape[1]] = value.reshape(joint.shape[0], ROWS, -1)
        at += own.shape[1]
    for own, got in ((out_small, (o2, o1, o3)), (in_small, (i2, i1, i3))):
        n = own.shape[1]
        small = total(own[...], [small_value(g[block:, 0 : 2 * n], n) for g in got])
        packed = small_rows(small, 2 * n)
        for i in range(joint.shape[0]):
            joint[i, :, at : at + 2 * n] = packed
        at += 2 * n


def last_kernel(scale, width, channels, joint, grad_in, grad_out, bias_out, loss, bias_in):
    n = joint.shape[0]

    def along(lo, hi):
        value = joint[0, :, lo:hi].astype(f32)
        for i in range(1, n):
            value = value + joint[i, :, lo:hi].astype(f32)
        return value

    grad_out[...] = along(0, channels) * scale
    at = channels + width
    grad_in[...] = along(channels, at) * scale
    small = (along(at, at + 256) + along(at + 256, at + 512)) * scale
    bias_out[...] = small[:, 0:128]
    loss[...] = -small[:, 128:256]
    at += 512
    bias_in[...] = (along(at, at + 128) + along(at + 128, at + 256)) * scale


def turn_kernel(dpre_t, dpre_pt, dpre, dpre_p):
    turn(dpre_pt, dpre_p)
    turn(dpre_t, dpre)


def hidden_kernel(dpre, dpre_r, w_mine, w_other, grad):
    def columns(at):
        grad[:, at] = (nn(dpre[...], w_mine[:, at]) + nn(dpre_r[...], w_other[:, at])).astype(bf16)

    whole = grad.shape[1] // 256

    @pl.loop(0, whole)
    def _(i):
        columns(pl.ds(pl.multiple_of(i * 256, 256), 256))

    if whole * 256 < grad.shape[1]:
        columns(slice(whole * 256, grad.shape[1]))


def on_device(hidden_states, teacher, proj_in, bias_in, proj_out, bias_out):
    samples, seq, width = hidden_states.shape
    units, channels = proj_out.shape
    ny, nx, nc, nz = (lax.axis_size(a) for a in DP_FEAT)
    z = lax.axis_index(Z)
    tokens = samples * seq
    block = units // (ny * nx * nc)
    half = units // nc
    share = block // nz
    scale = 1.0 / float(tokens * ny * nx * nc * nz)
    sems = pltpu.SemaphoreType.DMA((RING * RING,))
    one = 2 * half * tokens * channels

    rows = hidden_states.reshape(tokens, width)
    rows_p = shift(rows, C, 1)

    pieces = {0: lax.dynamic_slice_in_dim(teacher, z * samples, samples, 0)}
    for k in (4, 3, 5, 2, 6, 1, 7):
        to = lax.rem(z + k, nz)
        piece = lax.dynamic_slice_in_dim(teacher, to * samples, samples, 0)
        pieces[k] = shift(piece, Z, k)
    pieces = [pieces[k].reshape(tokens, channels // nz) for k in range(nz)]

    w_in = proj_in.reshape(ny, nx, nc, block, width)
    w_out = proj_out.reshape(ny, nx, nc, block, channels)

    act_t, act_pt, slope, slope_p, act, act_p, in_mine, in_other, out_mine, out_other = call(
        first_kernel,
        [VMEM, VMEM, HBM, HBM, VMEM],
        [((half, tokens), bf16)] * 2
        + [((half, tokens), f32)] * 2
        + [((tokens, half), bf16)] * 2
        + [((half, width), bf16)] * 2
        + [((half, channels), bf16)] * 2,
        [pltpu.VMEM((half, 1), f32), sems, sems, sems, sems],
        2 * one,
        40,
    )(rows, rows_p, w_in, w_out, bias_in[:, None])
    act_r = shift(act_p, C, 1)
    big = ((tokens, channels), f32)
    (out,) = call(out_kernel, [VMEM] * 3, [big], (), one)(act, out_mine, bias_out[None])
    (out,) = call(out_more_kernel, [VMEM] * 3, [big], (), one)(act_r, out_other, out)

    (cot,) = call(
        cot_kernel,
        [VMEM] * (1 + nz),
        [((tokens + ROWS, channels), bf16)],
        [pltpu.VMEM((8, 128), f32)],
        one // 4,
    )(out, *pieces)
    cot_p = shift(cot, C, 1)
    (dpre_t,) = call(back_kernel, [VMEM] * 3, [((half, tokens), bf16)], (), one)(
        cot, out_mine, slope
    )

    def messages(height, wide):
        return [((height + ROWS, wide), bf16)] * 3 + [((height, wide), f32)]

    quarter = RING * block
    *first, first_own, first_small, dpre_pt = call(
        grad_in_kernel,
        [VMEM] * 6,
        messages(quarter, width) + [((ROWS, 128), f32), ((half, tokens), bf16)],
        (),
        3 * one,
    )(cot_p, out_mine, slope_p, dpre_t, rows, rows_p)
    first = [shift(m, Y, k) for m, k in zip(first, SHIFTS)]

    *last, last_own, last_small = call(
        grad_out_kernel, [VMEM] * 4, messages(quarter, channels) + [((ROWS, 256), f32)], (), 2 * one
    )(act_t, act_pt, cot, cot_p)
    last = [shift(m, X, k) for m, k in zip(last, SHIFTS)]

    dpre, dpre_p = call(
        turn_kernel, [VMEM] * 2, [((tokens, half), bf16)] * 2, (), one
    )(dpre_t, dpre_pt)
    dpre_r = shift(dpre_p, C, 1)

    *first, first_own, first_small = call(
        functools.partial(middle_kernel, True),
        [VMEM] * 5,
        messages(block, width) + [((ROWS, 128), f32)],
        (),
        one // 8,
    )(first_own, first_small, *first)
    first = [shift(m, X, k) for m, k in zip(first, SHIFTS)]
    *last, last_own, last_small = call(
        functools.partial(middle_kernel, False),
        [VMEM] * 5,
        messages(block, channels) + [((ROWS, 256), f32)],
        (),
        one // 8,
    )(last_own, last_small, *last)
    last = [shift(m, Y, k) for m, k in zip(last, SHIFTS)]

    (joint,) = call(
        joint_kernel, [VMEM] * 10, [((nz, share, channels + width + 768), bf16)], (), one // 8
    )(last_own, last_small, *last, first_own, first_small, *first)
    dpre_r, joint = lax.optimization_barrier((dpre_r, joint))
    joint = lax.all_to_all(joint, Z, split_axis=0, concat_axis=0, tiled=True)
    (grad_hidden,) = call(
        hidden_kernel, [VMEM] * 4, [((tokens, width), bf16)], (), 2 * one
    )(dpre, dpre_r, in_mine, in_other)
    grad_in, grad_out, grad_bias_out, loss, grad_bias_in = call(
        functools.partial(last_kernel, scale, width, channels),
        [VMEM],
        [((share, width), f32), ((share, channels), f32)] + [((ROWS, 128), f32)] * 3,
    )(joint)
    return (
        grad_in,
        lax.dynamic_slice_in_dim(grad_bias_in[0], z * share, share, 0),
        grad_out,
        grad_bias_out.reshape(channels),
        grad_hidden.reshape(samples, seq, width),
        loss[0, 0],
    )


def solution(mesh):
    finer = Mesh(mesh.devices.reshape(4, 4, 2, mesh.shape["feat"]), DP_FEAT)
    return jax.shard_map(
        on_device,
        mesh=finer,
        in_specs=(P(DP_FEAT, None, None), P(DP, None, Z), P(), P(), P(), P()),
        out_specs=(
            P(DP_FEAT, None),
            P(DP_FEAT),
            P(DP_FEAT, None),
            P(),
            P(DP_FEAT, None, None),
            P(),
        ),
        check_vma=False,
    )
```

time: 379 us -> 150 us (0.40)
  waiting for transfers between devices: 245 us -> 48.4 us
  blocking collectives: 65.3 us -> 0 us
  Pallas kernels: 0 us -> 39.5 us
  starting transfers between devices: 8.65 us -> 41.1 us
  matrix products: 28.7 us -> 0 us
  local copies, waits for them, and re-layouts: 3.13 us -> 19 us
  between operations: 16 us -> 0.84 us
  other arithmetic: 12.2 us -> 0 us
    unnamed x2 -> x0, waiting for transfers between devices: 223 us -> none
    psum x4 -> x0, blocking collectives: 65.3 us -> none  [by_axis(): return functools.reduce(lax.psum, axes, x)]
    ppermute x0 -> x23, waiting for transfers between devices: none -> 44.5 us  [shift(): return lax.ppermute(x, axis, [(i, (i + k) % n) for i in range(n)])]
    pallas_call x0 -> x13, Pallas kernels: none -> 39.5 us  [the longest x1 13.7 us: on_device(): call(first_kernel, [VMEM, VMEM, HBM, HBM, VMEM], [((half, tokens), bf16)]...]
    ppermute x0 -> x23, starting transfers between devices: none -> 36.3 us  [shift(): return lax.ppermute(x, axis, [(i, (i + k) % n) for i in range(n)])]
    dot_general x6 -> x0, matrix products: 28.7 us -> none  [the longest x1 6.76 us: on_device(): lax.dot_general(rows, proj_in, (((1,), (1,)), ((), ())), preferred_elemen...]
    all_to_all x1, waiting for transfers between devices: 21.9 us -> 3.84 us  [on_device(): joint = lax.all_to_all(joint, Z, split_axis=0, concat_axis=0, tiled=True)]
    unnamed x19 -> x46, local copies, waits for them, and re-layouts: 2.5 us -> 15.4 us
  transfers between devices with their start and end apart: 2 -> 24, of which waited for: 2 -> 15; matrix products, arithmetic and copies ran while one was open for 4% -> 2% of each run, Pallas kernels for 0% -> 13%
where the time goes in v1:
time: 150 us; the launch traced here: 149 us
  waiting for transfers between devices  48.4 us (32%)
  starting transfers between devices  41.1 us (27%)
  Pallas kernels  39.5 us (26%)
  local copies, waits for them, and re-layouts  19 us (13%)
    ppermute x23, waiting for transfers between devices, shift(): return lax.ppermute(x, axis, [(i, (i + k) % n) for i in range(n)])  44.5 us
    ppermute x23, starting transfers between devices, shift(): return lax.ppermute(x, axis, [(i, (i + k) % n) for i in range(n)])  36.3 us
    unnamed x46, local copies, waits for them, and re-layouts  15.4 us
    pallas_call x1, Pallas kernels, on_device(): call(first_kernel, [VMEM, VMEM, HBM, HBM, VMEM], [((half, tokens), bf16)]...  13.7 us
    pallas_call x1, Pallas kernels, on_device(): call(grad_in_kernel, [VMEM] * 6, messages(quarter, width) + [((ROWS, 128)...  5.72 us
    all_to_all x1, starting transfers between devices, on_device(): joint = lax.all_to_all(joint, Z, split_axis=0, concat_axis=0, tiled=True)  4.85 us
    pallas_call x1, Pallas kernels, on_device(): call(hidden_kernel, [VMEM] * 4, [((tokens, width), bf16)], (), 2 * one)  4.61 us
    all_to_all x1, waiting for transfers between devices, on_device(): joint = lax.all_to_all(joint, Z, split_axis=0, concat_axis=0, tiled=True)  3.84 us
  transfers between devices with their start and end apart: 24, of which 15 were waited for; matrix products, arithmetic and copies ran while one was open for 2% of the time, Pallas kernels for 13%

profile of v1, /device:TPU:6, one launch (start us, length us, event | category | flops | bytes accessed | tf_op | source)
XLA Modules:
  0.0 148.8 jit_solution(7564111978800257351)
XLA Ops:
  1.8 2.0 %collective-permute-done.rows_p = bf16[512,1152]{1,0:T(8,128)(2,1)S(1)} collective-permute-done((bf16[512,1152]{1,0:T(8,128)(2,1)}, bf16[512,1152]{1,0:T(8,128)(2,1)S(1)}, u32[]{:S(2)}, u32[]{:S(2)}) %collective-permute-start) | collective-permute-done | bytes 1179680 | tf_op jit(solution)/shard_map/ppermute | solution.py:29
  7.3 13.7 %shard_map.109 = (bf16[1024,512]{1,0:T(8,128)(2,1)S(1)}, bf16[1024,512]{1,0:T(8,128)(2,1)S(1)}, f32[1024,512]{1,0:T(8,128)S(1)}, f32[1024,512]{1,0:T(8,128)S(1)}...) custom-call(bf16[512,1152]{1,0:T(8,128)(2,1)S(1)} %bitcast.19, ...), custom_call_target="tpu_custom_call" | custom-call | flops 2147483648 | bytes 4194304 | tf_op jit(solution)/shard_map/pallas_call | solution.py:375
  28.3 2.0 %collective-permute-start.2 = (bf16[2,256,128]{2,1,0:T(8,128)(2,1)S(1)}, bf16[2,256,128]{2,1,0:T(8,128)(2,1)S(1)}, u32[]{:S(2)}, u32[]{:S(2)}) collective-permute-start(bf16[2,256,128]{2,1,0:T(8,128)(2,1)S(1)} %get-tuple-element.91), channel_id=1, source_target_pairs={{0,1},{1,2},{2,3},{3,4},{4,5},{5,6},{6,7},{7,0},{8,9},{9,10},{10,1... | collective-permute-start | bytes 393224 | tf_op jit(solution)/shard_map/ppermute | solution.py:29
  30.3 3.3 %collective-permute-start.3 = (bf16[2,256,128]{2,1,0:T(8,128)(2,1)S(1)}, bf16[2,256,128]{2,1,0:T(8,128)(2,1)S(1)}, u32[]{:S(2)}, u32[]{:S(2)}) collective-permute-start(bf16[2,256,128]{2,1,0:T(8,128)(2,1)S(1)} %get-tuple-element.90), channel_id=1, source_target_pairs={{0,2},{1,3},{2,4},{3,5},{4,6},{5,7},{6,0},{7,1},{8,10},{9,11},{10,... | collective-permute-start | bytes 393224 | tf_op jit(solution)/shard_map/ppermute | solution.py:29
  33.6 4.0 %collective-permute-start.4 = (bf16[2,256,128]{2,1,0:T(8,128)(2,1)S(1)}, bf16[2,256,128]{2,1,0:T(8,128)(2,1)S(1)}, u32[]{:S(2)}, u32[]{:S(2)}) collective-permute-start(bf16[2,256,128]{2,1,0:T(8,128)(2,1)S(1)} %get-tuple-element.89), channel_id=1, source_target_pairs={{0,3},{1,4},{2,5},{3,6},{4,7},{5,0},{6,1},{7,2},{8,11},{9,12},{10,... | collective-permute-start | bytes 393224 | tf_op jit(solution)/shard_map/ppermute | solution.py:29
  38.6 4.5 %collective-permute-start.6 = (bf16[2,256,128]{2,1,0:T(8,128)(2,1)S(1)}, bf16[2,256,128]{2,1,0:T(8,128)(2,1)S(1)}, u32[]{:S(2)}, u32[]{:S(2)}) collective-permute-start(bf16[2,256,128]{2,1,0:T(8,128)(2,1)S(1)} %get-tuple-element.87), channel_id=1, source_target_pairs={{0,5},{1,6},{2,7},{3,0},{4,1},{5,2},{6,3},{7,4},{8,13},{9,14},{10,... | collective-permute-start | bytes 393224 | tf_op jit(solution)/shard_map/ppermute | solution.py:29
  43.1 3.5 %collective-permute-done.3 = bf16[2,256,128]{2,1,0:T(8,128)(2,1)S(1)} collective-permute-done((bf16[2,256,128]{2,1,0:T(8,128)(2,1)S(1)}, bf16[2,256,128]{2,1,0:T(8,128)(2,1)S(1)}, u32[]{:S(2)}, u32[]{:S(2)}) %collective-permute-start.3) | collective-permute-done | bytes 131104 | tf_op jit(solution)/shard_map/ppermute | solution.py:29
  46.6 3.4 %collective-permute-start.8 = (bf16[2,256,128]{2,1,0:T(8,128)(2,1)S(1)}, bf16[2,256,128]{2,1,0:T(8,128)(2,1)S(1)}, u32[]{:S(2)}, u32[]{:S(2)}) collective-permute-start(bf16[2,256,128]{2,1,0:T(8,128)(2,1)S(1)} %get-tuple-element.86), channel_id=1, source_target_pairs={{0,7},{1,0},{2,1},{3,2},{4,3},{5,4},{6,5},{7,6},{8,15},{9,8},{10,9... | collective-permute-start | bytes 393224 | tf_op jit(solution)/shard_map/ppermute | solution.py:29
  50.0 1.8 %shard_map.110.before = f32[512,1024]{1,0:T(8,128)S(1)} custom-call(bf16[512,1024]{1,0:T(8,128)(2,1)S(1)} %copy-done.15, bf16[1024,1024]{1,0:T(8,128)(2,1)S(1)} %get-tuple-element.49.w.w_mine, f32[1,1024]{1,0:T(1,128)S(1)} %bitcast.29), custom_call_target="tpu_custom_call" | custom-call | flops 1073741824 | bytes 4194304 | tf_op jit(solution)/shard_map/pallas_call | solution.py:389
  53.6 2.0 %collective-permute-done.4 = bf16[2,256,128]{2,1,0:T(8,128)(2,1)S(1)} collective-permute-done((bf16[2,256,128]{2,1,0:T(8,128)(2,1)S(1)}, bf16[2,256,128]{2,1,0:T(8,128)(2,1)S(1)}, u32[]{:S(2)}, u32[]{:S(2)}) %collective-permute-start.4) | collective-permute-done | bytes 131104 | tf_op jit(solution)/shard_map/ppermute | solution.py:29
  55.6 3.1 %collective-permute-done.6 = bf16[2,256,128]{2,1,0:T(8,128)(2,1)S(1)} collective-permute-done((bf16[2,256,128]{2,1,0:T(8,128)(2,1)S(1)}, bf16[2,256,128]{2,1,0:T(8,128)(2,1)S(1)}, u32[]{:S(2)}, u32[]{:S(2)}) %collective-permute-start.6) | collective-permute-done | bytes 131104 | tf_op jit(solution)/shard_map/ppermute | solution.py:29
  58.7 3.8 %collective-permute-done.7 = bf16[2,256,128]{2,1,0:T(8,128)(2,1)S(1)} collective-permute-done((bf16[2,256,128]{2,1,0:T(8,128)(2,1)S(1)}, bf16[2,256,128]{2,1,0:T(8,128)(2,1)S(1)}, u32[]{:S(2)}, u32[]{:S(2)}) %collective-permute-start.7) | collective-permute-done | bytes 131104 | tf_op jit(solution)/shard_map/ppermute | solution.py:29
  63.3 2.4 %shard_map.112.cot = bf16[520,1024]{1,0:T(8,128)(2,1)S(1)} custom-call(f32[512,1024]{1,0:T(8,128)S(1)} %shard_map.111.out, bf16[512,128]{1,0:T(8,128)(2,1)S(1)} %bitcast.21, bf16[512,128]{1,0:T(8,128)(2,1)S(1)} %bitcast.22, bf16[512,128]{1,0:T(8,128)(2,1)S(1)} %bitcast.23, bf16[512,128]{1,0:T(8,128)(2,1)S(1)} %bitcast.24, bf16[512,128]{1,0:T(8,128)(2,1)S(1)} %bitcast.25, ...), custom_call_target="tpu_custom_call" | custom-call | flops 268435456 | bytes 4194304 | tf_op jit(solution)/shard_map/pallas_call | solution.py:392
  68.5 3.3 %shard_map.116 = (bf16[264,1024]{1,0:T(8,128)(2,1)S(1)}, bf16[264,1024]{1,0:T(8,128)(2,1)S(1)}, bf16[264,1024]{1,0:T(8,128)(2,1)S(1)}, f32[256,1024]{1,0:T(8,128)S(1)}, f32[8,256]{1,0:T(8,128)S(1)}) custom-call(bf16[1024,512]{1,0:T(8,128)(2,1)S(1)} %copy-done.20, bf16[1024,512]{1,0:T(8,128)(2,1)S(1)} %copy-done.22, bf16[520,1024]{1,0:T(8,128)(2,1)S(1)} %shard_map.112.cot, ...), custom_call_target="tpu_custom_call" | custom-call | flops 2147483648 | bytes 4194304 | tf_op jit(solution)/shard_map/pallas_call | solution.py:417
  74.1 5.7 %shard_map.114 = (bf16[264,1152]{1,0:T(8,128)(2,1)S(1)}, bf16[264,1152]{1,0:T(8,128)(2,1)S(1)}, bf16[264,1152]{1,0:T(8,128)(2,1)S(1)}, f32[256,1152]{1,0:T(8,128...) custom-call(bf16[520,1024]{1,0:T(8,128)(2,1)S(1)} %collective-permute-done.9.cot_p, ...), custom_call_target="tpu_custom_call" | custom-call | flops 3221225472 | bytes 4194304 | tf_op jit(solution)/shard_map/pallas_call | solution.py:408
  79.8 2.7 %shard_map.115 = (bf16[512,1024]{1,0:T(8,128)(2,1)S(1)}, bf16[512,1024]{1,0:T(8,128)(2,1)S(1)}) custom-call(bf16[1024,512]{1,0:T(8,128)(2,1)S(1)} %shard_map.113.dpre.dpre_t, bf16[1024,512]{1,0:T(8,128)(2,1)S(1)} %get-tuple-element.52.dpre_pt), custom_call_target="tpu_custom_call" | custom-call | flops 1073741824 | bytes 4194304 | tf_op jit(solution)/shard_map/pallas_call | solution.py:422
  86.5 3.0 %collective-permute-start.18 = (bf16[264,1152]{1,0:T(8,128)(2,1)S(1)}, bf16[264,1152]{1,0:T(8,128)(2,1)S(1)}, u32[]{:S(2)}, u32[]{:S(2)}) collective-permute-start(bf16[264,1152]{1,0:T(8,128)(2,1)S(1)} %get-tuple-element.69), channel_id=1, source_target_pairs={{0,192},{64,0},{128,64},{192,128},{1,193},{65,1},{129,65},{193,129... | collective-permute-start | bytes 1824776 | tf_op jit(solution)/shard_map/ppermute | solution.py:29
  91.0 10.0 %collective-permute-done.13.g_c = bf16[264,1024]{1,0:T(8,128)(2,1)S(1)} collective-permute-done((bf16[264,1024]{1,0:T(8,128)(2,1)S(1)}, bf16[264,1024]{1,0:T(8,128)(2,1)S(1)}, u32[]{:S(2)}, u32[]{:S(2)}) %collective-permute-start.13) | collective-permute-done | bytes 540704 | tf_op jit(solution)/shard_map/ppermute | solution.py:29
  104.6 10.9 %collective-permute-done.18.g_b = bf16[264,1152]{1,0:T(8,128)(2,1)S(1)} collective-permute-done((bf16[264,1152]{1,0:T(8,128)(2,1)S(1)}, bf16[264,1152]{1,0:T(8,128)(2,1)S(1)}, u32[]{:S(2)}, u32[]{:S(2)}) %collective-permute-start.18) | collective-permute-done | bytes 608288 | tf_op jit(solution)/shard_map/ppermute | solution.py:29
  115.9 1.8 %collective-permute-start.20 = (bf16[72,1152]{1,0:T(8,128)(2,1)S(1)}, bf16[72,1152]{1,0:T(8,128)(2,1)S(1)}, u32[]{:S(2)}, u32[]{:S(2)}) collective-permute-start(bf16[72,1152]{1,0:T(8,128)(2,1)S(1)} %get-tuple-element.73), channel_id=1, source_target_pairs={{0,16},{16,32},{32,48},{48,0},{1,17},{17,33},{33,49},{49,1},{2,18}... | collective-permute-start | bytes 497672 | tf_op jit(solution)/shard_map/ppermute | solution.py:29
  121.2 5.5 %collective-permute-done.16.o3 = bf16[72,1024]{1,0:T(8,128)(2,1)S(1)} collective-permute-done((bf16[72,1024]{1,0:T(8,128)(2,1)S(1)}, bf16[72,1024]{1,0:T(8,128)(2,1)S(1)}, u32[]{:S(2)}, u32[]{:S(2)}) %collective-permute-start.16) | collective-permute-done | bytes 147488 | tf_op jit(solution)/shard_map/ppermute | solution.py:29
  129.7 4.8 %all-to-all-start = ((bf16[8,8,2944]{2,1,0:T(8,128)(2,1)}), bf16[8,8,2944]{2,1,0:T(8,128)(2,1)S(1)}, u32[]{:S(2)}, u32[]{:S(2)}) async-start(bf16[8,8,2944]{2,1,0:T(8,128)(2,1)} %shard_map.119), calls=%async_computation | async-start | bytes 753664 | tf_op jit(solution)/shard_map/all_to_all | solution.py:448
  138.6 4.6 %shard_map.121 = bf16[512,1152]{1,0:T(8,128)(2,1)} custom-call(bf16[512,1024]{1,0:T(8,128)(2,1)S(1)} %copy-done.11, bf16[512,1024]{1,0:T(8,128)(2,1)S(1)} %copy-done.13, bf16[1024,1152]{1,0:T(8,128)(2,1)S(1)} %copy-done, bf16[1024,1152]{1,0:T(8,128)(2,1)S(1)} %copy-done.1), custom_call_target="tpu_custom_call" | custom-call | flops 2147483648 | bytes 4194304 | tf_op jit(solution)/shard_map/pallas_call | solution.py:449
  143.2 3.8 %all-to-all-done.joint = bf16[8,8,2944]{2,1,0:T(8,128)(2,1)S(1)} async-done(((bf16[8,8,2944]{2,1,0:T(8,128)(2,1)}), bf16[8,8,2944]{2,1,0:T(8,128)(2,1)S(1)}, u32[]{:S(2)}, u32[]{:S(2)}) %all-to-all-start) | async-done | bytes 376864 | tf_op jit(solution)/shard_map/all_to_all | solution.py:448
  (88 shorter events, 42.6 us)
Async XLA Ops:
  0.6 3.1 %collective-permute-start = (bf16[512,1152]{1,0:T(8,128)(2,1)}, bf16[512,1152]{1,0:T(8,128)(2,1)S(1)}, u32[]{:S(2)}, u32[]{:S(2)}) collective-permute-start(bf16[512,1152]{1,0:T(8,128)(2,1)} %bitcast.18), channel_id=1, source_target_pairs={{0,8},{8,0},{1,9},{9,1},{2,10},{10,2},{3,11},{11,3},{4,12},{12,4},... | collective-permute-start | bytes 3538952 | tf_op jit(solution)/shard_map/ppermute | solution.py:29
  26.7 19.9 %collective-permute-start.1 = (bf16[512,1024]{1,0:T(8,128)(2,1)}, bf16[512,1024]{1,0:T(8,128)(2,1)S(1)}, u32[]{:S(2)}, u32[]{:S(2)}) collective-permute-start(bf16[512,1024]{1,0:T(8,128)(2,1)} %get-tuple-element.46), channel_id=1, source_target_pairs={{0,8},{8,0},{1,9},{9,1},{2,10},{10,2},{3,11},{11,3},{4,12},{12,4},... | collective-permute-start | bytes 3145736 | tf_op jit(solution)/shard_map/ppermute | solution.py:29
  28.3 10.3 %collective-permute-start.2 = (bf16[2,256,128]{2,1,0:T(8,128)(2,1)S(1)}, bf16[2,256,128]{2,1,0:T(8,128)(2,1)S(1)}, u32[]{:S(2)}, u32[]{:S(2)}) collective-permute-start(bf16[2,256,128]{2,1,0:T(8,128)(2,1)S(1)} %get-tuple-element.91), channel_id=1, source_target_pairs={{0,1},{1,2},{2,3},{3,4},{4,5},{5,6},{6,7},{7,0},{8,9},{9,10},{10,1... | collective-permute-start | bytes 393224 | tf_op jit(solution)/shard_map/ppermute | solution.py:29
  30.3 16.3 %collective-permute-start.3 = (bf16[2,256,128]{2,1,0:T(8,128)(2,1)S(1)}, bf16[2,256,128]{2,1,0:T(8,128)(2,1)S(1)}, u32[]{:S(2)}, u32[]{:S(2)}) collective-permute-start(bf16[2,256,128]{2,1,0:T(8,128)(2,1)S(1)} %get-tuple-element.90), channel_id=1, source_target_pairs={{0,2},{1,3},{2,4},{3,5},{4,6},{5,7},{6,0},{7,1},{8,10},{9,11},{10,... | collective-permute-start | bytes 393224 | tf_op jit(solution)/shard_map/ppermute | solution.py:29
  33.6 22.0 %collective-permute-start.4 = (bf16[2,256,128]{2,1,0:T(8,128)(2,1)S(1)}, bf16[2,256,128]{2,1,0:T(8,128)(2,1)S(1)}, u32[]{:S(2)}, u32[]{:S(2)}) collective-permute-start(bf16[2,256,128]{2,1,0:T(8,128)(2,1)S(1)} %get-tuple-element.89), channel_id=1, source_target_pairs={{0,3},{1,4},{2,5},{3,6},{4,7},{5,0},{6,1},{7,2},{8,11},{9,12},{10,... | collective-permute-start | bytes 393224 | tf_op jit(solution)/shard_map/ppermute | solution.py:29
  37.6 18.0 %collective-permute-start.5 = (bf16[2,256,128]{2,1,0:T(8,128)(2,1)S(1)}, bf16[2,256,128]{2,1,0:T(8,128)(2,1)S(1)}, u32[]{:S(2)}, u32[]{:S(2)}) collective-permute-start(bf16[2,256,128]{2,1,0:T(8,128)(2,1)S(1)} %get-tuple-element.88), channel_id=1, source_target_pairs={{0,4},{1,5},{2,6},{3,7},{4,0},{5,1},{6,2},{7,3},{8,12},{9,13},{10,... | collective-permute-start | bytes 393224 | tf_op jit(solution)/shard_map/ppermute | solution.py:29
  38.6 20.1 %collective-permute-start.6 = (bf16[2,256,128]{2,1,0:T(8,128)(2,1)S(1)}, bf16[2,256,128]{2,1,0:T(8,128)(2,1)S(1)}, u32[]{:S(2)}, u32[]{:S(2)}) collective-permute-start(bf16[2,256,128]{2,1,0:T(8,128)(2,1)S(1)} %get-tuple-element.87), channel_id=1, source_target_pairs={{0,5},{1,6},{2,7},{3,0},{4,1},{5,2},{6,3},{7,4},{8,13},{9,14},{10,... | collective-permute-start | bytes 393224 | tf_op jit(solution)/shard_map/ppermute | solution.py:29
  46.6 15.8 %collective-permute-start.7 = (bf16[2,256,128]{2,1,0:T(8,128)(2,1)S(1)}, bf16[2,256,128]{2,1,0:T(8,128)(2,1)S(1)}, u32[]{:S(2)}, u32[]{:S(2)}) collective-permute-start(bf16[2,256,128]{2,1,0:T(8,128)(2,1)S(1)} %get-tuple-element.93), channel_id=1, source_target_pairs={{0,6},{1,7},{2,0},{3,1},{4,2},{5,3},{6,4},{7,5},{8,14},{9,15},{10,... | collective-permute-start | bytes 393224 | tf_op jit(solution)/shard_map/ppermute | solution.py:29
  46.6 16.7 %collective-permute-start.8 = (bf16[2,256,128]{2,1,0:T(8,128)(2,1)S(1)}, bf16[2,256,128]{2,1,0:T(8,128)(2,1)S(1)}, u32[]{:S(2)}, u32[]{:S(2)}) collective-permute-start(bf16[2,256,128]{2,1,0:T(8,128)(2,1)S(1)} %get-tuple-element.86), channel_id=1, source_target_pairs={{0,7},{1,0},{2,1},{3,2},{4,3},{5,4},{6,5},{7,6},{8,15},{9,8},{10,9... | collective-permute-start | bytes 393224 | tf_op jit(solution)/shard_map/ppermute | solution.py:29
  65.7 2.8 %collective-permute-start.9 = (bf16[520,1024]{1,0:T(8,128)(2,1)S(1)}, bf16[520,1024]{1,0:T(8,128)(2,1)S(1)}, u32[]{:S(2)}, u32[]{:S(2)}) collective-permute-start(bf16[520,1024]{1,0:T(8,128)(2,1)S(1)} %shard_map.112.cot), channel_id=1, source_target_pairs={{0,8},{8,0},{1,9},{9,1},{2,10},{10,2},{3,11},{11,3},{4,12},{12,4},... | collective-permute-start | bytes 3194888 | tf_op jit(solution)/shard_map/ppermute | solution.py:29
  71.8 14.7 %collective-permute-start.11 = (bf16[264,1024]{1,0:T(8,128)(2,1)S(1)}, bf16[264,1024]{1,0:T(8,128)(2,1)S(1)}, u32[]{:S(2)}, u32[]{:S(2)}) collective-permute-start(bf16[264,1024]{1,0:T(8,128)(2,1)S(1)} %get-tuple-element.58), channel_id=1, source_target_pairs={{0,16},{16,32},{32,48},{48,0},{1,17},{17,33},{33,49},{49,1},{2,18}... | collective-permute-start | bytes 1622024 | tf_op jit(solution)/shard_map/ppermute | solution.py:29
  72.6 16.8 %collective-permute-start.12 = (bf16[264,1024]{1,0:T(8,128)(2,1)S(1)}, bf16[264,1024]{1,0:T(8,128)(2,1)S(1)}, u32[]{:S(2)}, u32[]{:S(2)}) collective-permute-start(bf16[264,1024]{1,0:T(8,128)(2,1)S(1)} %get-tuple-element.59), channel_id=1, source_target_pairs={{0,48},{16,0},{32,16},{48,32},{1,49},{17,1},{33,17},{49,33},{2,50}... | collective-permute-start | bytes 1622024 | tf_op jit(solution)/shard_map/ppermute | solution.py:29
  83.4 45.2 %collective-permute-start.10 = (bf16[512,1024]{1,0:T(8,128)(2,1)S(1)}, bf16[512,1024]{1,0:T(8,128)(2,1)S(1)}, u32[]{:S(2)}, u32[]{:S(2)}) collective-permute-start(bf16[512,1024]{1,0:T(8,128)(2,1)S(1)} %get-tuple-element.53), channel_id=1, source_target_pairs={{0,8},{8,0},{1,9},{9,1},{2,10},{10,2},{3,11},{11,3},{4,12},{12,4},... | collective-permute-start | bytes 3145736 | tf_op jit(solution)/shard_map/ppermute | solution.py:29
  83.4 19.4 %collective-permute-start.17 = (bf16[264,1152]{1,0:T(8,128)(2,1)S(1)}, bf16[264,1152]{1,0:T(8,128)(2,1)S(1)}, u32[]{:S(2)}, u32[]{:S(2)}) collective-permute-start(bf16[264,1152]{1,0:T(8,128)(2,1)S(1)} %get-tuple-element.68), channel_id=1, source_target_pairs={{0,64},{64,128},{128,192},{192,0},{1,65},{65,129},{129,193},{193,1... | collective-permute-start | bytes 1824776 | tf_op jit(solution)/shard_map/ppermute | solution.py:29
  85.1 15.9 %collective-permute-start.13 = (bf16[264,1024]{1,0:T(8,128)(2,1)S(1)}, bf16[264,1024]{1,0:T(8,128)(2,1)S(1)}, u32[]{:S(2)}, u32[]{:S(2)}) collective-permute-start(bf16[264,1024]{1,0:T(8,128)(2,1)S(1)} %get-tuple-element.60), channel_id=1, source_target_pairs={{0,32},{16,48},{32,0},{48,16},{1,33},{17,49},{33,1},{49,17},{2,34}... | collective-permute-start | bytes 1622024 | tf_op jit(solution)/shard_map/ppermute | solution.py:29
  86.5 29.0 %collective-permute-start.18 = (bf16[264,1152]{1,0:T(8,128)(2,1)S(1)}, bf16[264,1152]{1,0:T(8,128)(2,1)S(1)}, u32[]{:S(2)}, u32[]{:S(2)}) collective-permute-start(bf16[264,1152]{1,0:T(8,128)(2,1)S(1)} %get-tuple-element.69), channel_id=1, source_target_pairs={{0,192},{64,0},{128,64},{192,128},{1,193},{65,1},{129,65},{193,129... | collective-permute-start | bytes 1824776 | tf_op jit(solution)/shard_map/ppermute | solution.py:29
  89.4 26.2 %collective-permute-start.19 = (bf16[264,1152]{1,0:T(8,128)(2,1)S(1)}, bf16[264,1152]{1,0:T(8,128)(2,1)S(1)}, u32[]{:S(2)}, u32[]{:S(2)}) collective-permute-start(bf16[264,1152]{1,0:T(8,128)(2,1)S(1)} %get-tuple-element.70), channel_id=1, source_target_pairs={{0,128},{64,192},{128,0},{192,64},{1,129},{65,193},{129,1},{193,65... | collective-permute-start | bytes 1824776 | tf_op jit(solution)/shard_map/ppermute | solution.py:29
  101.3 17.0 %collective-permute-start.14 = (bf16[72,1024]{1,0:T(8,128)(2,1)S(1)}, bf16[72,1024]{1,0:T(8,128)(2,1)S(1)}, u32[]{:S(2)}, u32[]{:S(2)}) collective-permute-start(bf16[72,1024]{1,0:T(8,128)(2,1)S(1)} %get-tuple-element.63), channel_id=1, source_target_pairs={{0,64},{64,128},{128,192},{192,0},{1,65},{65,129},{129,193},{193,1... | collective-permute-start | bytes 442376 | tf_op jit(solution)/shard_map/ppermute | solution.py:29
  102.9 16.8 %collective-permute-start.15 = (bf16[72,1024]{1,0:T(8,128)(2,1)S(1)}, bf16[72,1024]{1,0:T(8,128)(2,1)S(1)}, u32[]{:S(2)}, u32[]{:S(2)}) collective-permute-start(bf16[72,1024]{1,0:T(8,128)(2,1)S(1)} %get-tuple-element.64), channel_id=1, source_target_pairs={{0,192},{64,0},{128,64},{192,128},{1,193},{65,1},{129,65},{193,129... | collective-permute-start | bytes 442376 | tf_op jit(solution)/shard_map/ppermute | solution.py:29
  115.9 10.8 %collective-permute-start.20 = (bf16[72,1152]{1,0:T(8,128)(2,1)S(1)}, bf16[72,1152]{1,0:T(8,128)(2,1)S(1)}, u32[]{:S(2)}, u32[]{:S(2)}) collective-permute-start(bf16[72,1152]{1,0:T(8,128)(2,1)S(1)} %get-tuple-element.73), channel_id=1, source_target_pairs={{0,16},{16,32},{32,48},{48,0},{1,17},{17,33},{33,49},{49,1},{2,18}... | collective-permute-start | bytes 497672 | tf_op jit(solution)/shard_map/ppermute | solution.py:29
  117.7 10.1 %collective-permute-start.21 = (bf16[72,1152]{1,0:T(8,128)(2,1)S(1)}, bf16[72,1152]{1,0:T(8,128)(2,1)S(1)}, u32[]{:S(2)}, u32[]{:S(2)}) collective-permute-start(bf16[72,1152]{1,0:T(8,128)(2,1)S(1)} %get-tuple-element.74), channel_id=1, source_target_pairs={{0,48},{16,0},{32,16},{48,32},{1,49},{17,1},{33,17},{49,33},{2,50}... | collective-permute-start | bytes 497672 | tf_op jit(solution)/shard_map/ppermute | solution.py:29
  118.3 9.5 %collective-permute-start.22 = (bf16[72,1152]{1,0:T(8,128)(2,1)S(1)}, bf16[72,1152]{1,0:T(8,128)(2,1)S(1)}, u32[]{:S(2)}, u32[]{:S(2)}) collective-permute-start(bf16[72,1152]{1,0:T(8,128)(2,1)S(1)} %get-tuple-element.75), channel_id=1, source_target_pairs={{0,32},{16,48},{32,0},{48,16},{1,33},{17,49},{33,1},{49,17},{2,34}... | collective-permute-start | bytes 497672 | tf_op jit(solution)/shard_map/ppermute | solution.py:29
  119.7 7.0 %collective-permute-start.16 = (bf16[72,1024]{1,0:T(8,128)(2,1)S(1)}, bf16[72,1024]{1,0:T(8,128)(2,1)S(1)}, u32[]{:S(2)}, u32[]{:S(2)}) collective-permute-start(bf16[72,1024]{1,0:T(8,128)(2,1)S(1)} %get-tuple-element.65), channel_id=1, source_target_pairs={{0,128},{64,192},{128,0},{192,64},{1,129},{65,193},{129,1},{193,65... | collective-permute-start | bytes 442376 | tf_op jit(solution)/shard_map/ppermute | solution.py:29
  129.7 17.4 %all-to-all-start = ((bf16[8,8,2944]{2,1,0:T(8,128)(2,1)}), bf16[8,8,2944]{2,1,0:T(8,128)(2,1)S(1)}, u32[]{:S(2)}, u32[]{:S(2)}) async-start(bf16[8,8,2944]{2,1,0:T(8,128)(2,1)} %shard_map.119), calls=%async_computation | async-start | bytes 753664 | tf_op jit(solution)/shard_map/all_to_all | solution.py:448
  (23 other events, 107.0 us)

commit v2 on v1

v2 whole, which is shorter than its diff:
```python
import functools

import jax
import jax.numpy as jnp
from jax import lax
from jax.experimental import pallas as pl
from jax.experimental.pallas import tpu as pltpu
from jax.sharding import Mesh
from jax.sharding import PartitionSpec as P


Y, X, C, Z = "dp_0", "dp_1", "dp_2", "feat"
DP = (Y, X, C)
DP_FEAT = (Y, X, C, Z)

epsilon = 1e-06
f32, bf16 = jnp.float32, jnp.bfloat16
RING = 4
SHIFTS = (2, 3, 1)
TEACH = (7, 1, 6, 2, 5, 3, 4)
ROWS = 8
MIB = 1 << 20

VMEM = pl.BlockSpec(memory_space=pltpu.VMEM)
HBM = pl.BlockSpec(memory_space=pltpu.HBM)


def shift(x, axis, k):
    n = lax.axis_size(axis)
    return lax.ppermute(x, axis, [(i, (i + k) % n) for i in range(n)])


def shifts(xs, axis):
    return [shift(x, axis, k) for x, k in zip(xs, SHIFTS)]


def nt(a, b):
    return lax.dot_general(a, b, (((1,), (1,)), ((), ())), preferred_element_type=f32)


def nn(a, b):
    return jnp.dot(a, b, preferred_element_type=f32)


def high_low(v):
    high = v.astype(bf16)
    return high, (v - high.astype(f32)).astype(bf16)


def total(own, got):
    at2, at3, at1 = got
    return (own + at2) + (at1 + at3)


def call(body, ins, outs, scratch=(), flops=0, limit=16):
    return pl.pallas_call(
        body,
        out_shape=[jax.ShapeDtypeStruct(s, d) for s, d in outs],
        in_specs=ins,
        out_specs=[VMEM] * len(outs),
        scratch_shapes=list(scratch),
        compiler_params=pltpu.CompilerParams(vmem_limit_bytes=limit * MIB),
        cost_estimate=pl.CostEstimate(flops=flops, bytes_accessed=4 * MIB, transcendentals=0),
    )


def in_hbm(x):
    return pltpu.with_memory_space_constraint(x, pltpu.HBM)


def gather(w_ref, to_ref, sem, core):
    y, x = lax.axis_index(Y), lax.axis_index(X)
    block = w_ref.shape[3]
    for kx in range(RING):
        for ky in range(RING):
            pltpu.make_async_copy(
                w_ref.at[lax.rem(y + ky, RING), lax.rem(x + kx, RING), core],
                to_ref.at[pl.ds((kx * RING + ky) * block, block)],
                sem,
            ).start()
    return pltpu.make_async_copy(to_ref, to_ref, sem)


def identity(n):
    row = lax.broadcasted_iota(jnp.int32, (n, n), 0)
    return jnp.where(row == lax.broadcasted_iota(jnp.int32, (n, n), 1), 1.0, 0.0).astype(bf16)


def turn(ref, to):
    eye = identity(256)

    for i in range(0, ref.shape[0], 256):
        for j in range(0, ref.shape[1], 256):
            to[j : j + 256, i : i + 256] = nt(eye, ref[i : i + 256, j : j + 256]).astype(bf16)


def first_kernel(
    rows, rows_p, w_in, w_out, bias, act_t, act_pt, slope, slope_p, act, act_p, out_mine,
    out_other, in_mine, col, s0, s1, s2,
):
    y, x, c = lax.axis_index(Y), lax.axis_index(X), lax.axis_index(C)
    now = gather(w_in, in_mine, s0, c)
    later = [gather(w_out, out_mine, s1, c), gather(w_out, out_other, s2, 1 - c)]
    block = w_in.shape[3]
    for kx in range(RING):
        for ky in range(RING):
            of = (lax.rem(y + ky, RING) * RING + lax.rem(x + kx, RING)) * 2 + c
            col[pl.ds((kx * RING + ky) * block, block), :] = bias[
                pl.ds(pl.multiple_of(of * block, block), block), :
            ]
    now.wait()

    for r, a, s in ((rows, act_t, slope), (rows_p, act_pt, slope_p)):

        @pl.loop(0, r.shape[0] // 256)
        def _(i):
            at = pl.ds(pl.multiple_of(i * 256, 256), 256)
            pre = nt(in_mine[...], r[at, :]) + col[...]
            sig = jax.nn.sigmoid(pre)
            a[:, at] = (pre * sig).astype(bf16)
            s[:, at] = sig * (1.0 + pre * (1.0 - sig))

    turn(act_pt, act_p)
    turn(act_t, act)
    for copy in later:
        copy.wait()


def out_kernel(act, w, bias, out):
    @pl.loop(0, w.shape[1] // 256)
    def _(i):
        at = pl.ds(pl.multiple_of(i * 256, 256), 256)
        out[:, at] = nn(act[...], w[:, at]) + bias[:, at]


def out_more_kernel(act, w, before, out):
    @pl.loop(0, w.shape[1] // 256)
    def _(i):
        at = pl.ds(pl.multiple_of(i * 256, 256), 256)
        out[:, at] = before[:, at] + nn(act[...], w[:, at])


def split_kernel(distances, teacher, *refs):
    outs, sems = refs[:-1], refs[-1]
    z, n = lax.axis_index(Z), lax.axis_size(Z)
    tokens = outs[0].shape[0]
    copies = []
    for i, (k, out) in enumerate(zip(distances, outs)):
        of = pl.multiple_of(lax.rem(z + k, n) * tokens, tokens)
        copies.append(pltpu.make_async_copy(teacher.at[pl.ds(of, tokens)], out, sems.at[i]))
    for copy in copies:
        copy.start()
    for copy in copies:
        copy.wait()


def cot_kernel(out, *refs):
    given, (cot, total_ref, held, sems) = refs[:-4], refs[-4:]
    z = lax.axis_index(Z)
    n = len(given)
    tokens = out.shape[0]
    lanes = given[0].shape[1]
    part = tokens // 2
    for p in range(2):
        for k, piece in enumerate(given):
            rows = pl.ds(p * part, part)
            if k == 0:
                rows = pl.ds(pl.multiple_of(z * tokens + p * part, part), part)
            pltpu.make_async_copy(piece.at[rows], held.at[p, k], sems.at[p]).start()
    total_ref[...] = jnp.zeros_like(total_ref)
    step = 64

    def of(k):
        return pl.ds(pl.multiple_of(lax.rem(z - k + n, n) * lanes, lanes), lanes)

    for p in range(2):
        pltpu.make_async_copy(held.at[p], held.at[p], sems.at[p]).wait()

        @pl.loop(0, part // step)
        def _(i):
            of_part = pl.ds(pl.multiple_of(i * step, step), step)
            at = pl.ds(pl.multiple_of(p * part + i * step, step), step)
            zz = yy = zy = jnp.zeros((step, lanes), f32)
            for k in range(n):
                o, t = out[at, of(k)], held[p, k, of_part, :].astype(f32)
                zz, yy, zy = zz + o * o, yy + t * t, zy + o * t
            zz, yy, zy = (jnp.sum(v, axis=1, keepdims=True) for v in (zz, yy, zy))
            norm_z = jnp.sqrt(zz + epsilon)
            norms = norm_z * jnp.sqrt(yy + epsilon)
            cosine = zy / norms
            total_ref[...] += jnp.sum(cosine)
            by_target = 1.0 / norms
            by_out = cosine / (norm_z * norm_z)
            for k in range(n):
                o, t = out[at, of(k)], held[p, k, of_part, :].astype(f32)
                cot[at, of(k)] = (by_out * o - t * by_target).astype(bf16)

    high, low = high_low(jnp.broadcast_to(total_ref[0:1, 0:1], (ROWS, cot.shape[1])))
    row = lax.broadcasted_iota(jnp.int32, high.shape, 0)
    cot[pl.ds(tokens, ROWS), :] = jnp.where(
        row == 0, high.astype(f32), jnp.where(row == 1, low.astype(f32), 0.0)
    ).astype(bf16)


def back_kernel(cot, w_mine, slope, dpre):
    @pl.loop(0, slope.shape[1] // 256)
    def _(i):
        at = pl.ds(pl.multiple_of(i * 256, 256), 256)
        dpre[:, at] = (nt(w_mine[...], cot[at, :]) * slope[:, at]).astype(bf16)


def small_rows(value, width):
    high, low = high_low(value)
    pad = width - 2 * value.shape[1]
    rest = [jnp.zeros((ROWS, pad), bf16)] if pad else []
    return jnp.concatenate([high, low] + rest, axis=1)


def small_value(rows, n):
    rows = rows.astype(f32)
    return rows[:, :n] + rows[:, n : 2 * n]


def with_ones(ref, width):
    return jnp.concatenate([ref[:, width - 128 :], jnp.ones((ref.shape[0], 128), bf16)], axis=1)


def over_columns(width, product, write):
    whole = (width - 128) // 256
    assert width == whole * 256 + 128

    @pl.loop(0, whole)
    def _(j):
        at = pl.ds(pl.multiple_of(j * 256, 256), 256)
        write(product(lambda ref: ref[:, at]), at)

    value = product(lambda ref: with_ones(ref, width))
    write(value[:, :128], slice(width - 128, width))
    return value[:, 128:]


def bias_rows(sums, block):
    row = lax.broadcasted_iota(jnp.int32, (ROWS, 128), 0)
    unit = lax.broadcasted_iota(jnp.int32, (block, 128), 0)
    lane = lax.broadcasted_iota(jnp.int32, (block, 128), 1)
    small = jnp.zeros((ROWS, 128), f32)
    for kx, part in enumerate(sums):
        part = jnp.sum(jnp.where(unit == lane, part, 0.0), axis=0, keepdims=True)
        small = jnp.where(row == kx, part, small)
    return small


def blocks_of(k, block):
    return [slice((kx * RING + k) * block, (kx * RING + k + 1) * block) for kx in range(RING)]


def grad_in_far_kernel(cot_p, w_mine, slope_p, dpre, rows, rows_p, far, mine, partner):
    block = dpre.shape[0] // (RING * RING)
    tokens, width = rows.shape
    of = blocks_of(SHIFTS[0], block)
    weights = jnp.concatenate([w_mine[b, :] for b in of], axis=0)
    mine[...] = jnp.concatenate([dpre[b, :] for b in of], axis=0)
    slope = jnp.concatenate([slope_p[b, :] for b in of], axis=0)
    partner[...] = (nt(weights, cot_p[0:tokens, :]) * slope).astype(bf16)

    def write(value, at):
        far[0 : RING * block, at] = value.astype(bf16)

    sums = over_columns(
        width, lambda take: nn(mine[...], take(rows)) + nn(partner[...], take(rows_p)), write
    )
    small = bias_rows([sums[i * block : (i + 1) * block] for i in range(RING)], block)
    far[RING * block :, :] = small_rows(small, width)


def grad_in_kernel(cot_p, w_mine, slope_p, dpre, rows, rows_p, m_b, m_c, own, own_bias, dpre_p):
    back_kernel(cot_p, w_mine, slope_p, dpre_p)
    block = dpre.shape[0] // (RING * RING)
    width = rows.shape[1]
    turns = ((SHIFTS[1], m_b), (SHIFTS[2], m_c), (0, own))

    def write(value, at):
        for k, to in turns:
            for kx, b in enumerate(blocks_of(k, block)):
                to[kx * block : (kx + 1) * block, at] = value[b].astype(to.dtype)

    sums = over_columns(
        width, lambda take: nn(dpre[...], take(rows)) + nn(dpre_p[...], take(rows_p)), write
    )
    for k, to in turns:
        small = bias_rows([sums[b] for b in blocks_of(k, block)], block)
        if k:
            to[RING * block :, :] = small_rows(small, width)
        else:
            own_bias[...] = small


def grad_out_far_kernel(act, act_p, cot, cot_p, far, packed, own_small):
    tokens = act.shape[1]
    step = 256
    units = slice(SHIFTS[0] * step, (SHIFTS[0] + 1) * step)

    @pl.loop(0, cot.shape[1] // step)
    def _(j):
        at = pl.ds(pl.multiple_of(j * step, step), step)
        value = nn(act[units, :], cot[0:tokens, at]) + nn(act_p[units, :], cot_p[0:tokens, at])
        far[0:step, at] = value.astype(bf16)

    def sums(ref):
        return jnp.sum(ref[0:tokens, :].astype(f32), axis=0, keepdims=True)

    def cosines(ref):
        tail = ref[tokens : tokens + ROWS, 0:128].astype(f32)
        return tail[0:1] + tail[1:2]

    bias = sums(cot) + sums(cot_p)
    loss = cosines(cot) + cosines(cot_p)
    row = lax.broadcasted_iota(jnp.int32, (ROWS, 128), 0)
    small = jnp.zeros((ROWS, 128), f32)
    for r in range(ROWS):
        small = jnp.where(row == r, bias[:, r * 128 : (r + 1) * 128], small)
    small = jnp.concatenate([small, jnp.broadcast_to(loss, (ROWS, 128))], axis=1)
    value = small_rows(small, cot.shape[1])
    far[step:, :] = value
    packed[...] = value
    own_small[...] = small_value(value, 256)


def grad_out_kernel(act, act_p, cot, cot_p, packed, m_b, m_c, own):
    tokens = act.shape[1]
    step = 256
    near = {k: to for k, to in zip((*SHIFTS[1:], 0), (m_b, m_c, own))}

    @pl.loop(0, cot.shape[1] // step)
    def _(j):
        at = pl.ds(pl.multiple_of(j * step, step), step)
        a, b = cot[0:tokens, at], cot_p[0:tokens, at]
        for low, high in ((0, 2), (3, 4)):
            units = slice(low * step, high * step)
            value = nn(act[units, :], a) + nn(act_p[units, :], b)
            for k in range(low, high):
                part = value[(k - low) * step : (k - low + 1) * step]
                near[k][0:step, at] = part.astype(near[k].dtype)

    for to in (m_b, m_c):
        to[step:, :] = packed[...]


def middle_kernel(by_row, own, own_small, g_a, g_b, g_c, m_a, m_b, m_c, kept, kept_small):
    height = own.shape[0]
    block = height // RING
    width = own.shape[1]
    n = own_small.shape[1]
    got = (g_a, g_b, g_c)
    small = total(own_small[...], [small_value(g[height:, 0 : 2 * n], n) for g in got])
    packed = small_rows(small, width)
    for k, to in zip((*SHIFTS, 0), (m_a, m_b, m_c, kept)):
        at = pl.ds(k * block, block)
        value = total(own[at, :], [g[at, :].astype(f32) for g in got])
        to[0:block, :] = value.astype(to.dtype)
        if by_row:
            part = jnp.broadcast_to(small[k : k + 1], small.shape)
            if k:
                to[block:, :] = small_rows(part, width)
            else:
                kept_small[...] = part
        elif k:
            to[block:, :] = packed
        else:
            kept_small[...] = small_value(packed, n)


def joint_kernel(out_own, out_small, o2, o1, o3, in_own, in_small, i2, i1, i3, joint):
    block = out_own.shape[0]
    at = 0
    for own, got in ((out_own, (o2, o1, o3)), (in_own, (i2, i1, i3))):
        value = total(own[...], [g[0:block, :].astype(f32) for g in got]).astype(bf16)
        joint[:, :, at : at + own.shape[1]] = value.reshape(joint.shape[0], ROWS, -1)
        at += own.shape[1]
    sums = []
    for own, got in ((out_small, (o2, o1, o3)), (in_small, (i2, i1, i3))):
        n = own.shape[1]
        sums.append(total(own[...], [small_value(g[block:, 0 : 2 * n], n) for g in got]))
    high, low = high_low(jnp.concatenate(sums, axis=1))
    row = lax.broadcasted_iota(jnp.int32, (ROWS, 128), 0)
    terms = [v[:, j : j + 128].astype(f32) for j in (256, 128) for v in (high, low)]
    mixed = jnp.where(row == 0, terms[0], terms[1])
    mixed = jnp.where(row == 2, terms[2], jnp.where(row == 3, terms[3], mixed))
    packed = jnp.concatenate([high[:, :128], low[:, :128], mixed.astype(bf16)], axis=1)
    for i in range(joint.shape[0]):
        joint[i, :, at:] = packed


def last_kernel(scale, width, channels, joint, grad_in, grad_out, bias_out, loss, bias_in):
    n = joint.shape[0]

    def along(lo, hi):
        value = joint[0, :, lo:hi].astype(f32)
        for i in range(1, n):
            value = value + joint[i, :, lo:hi].astype(f32)
        return value

    grad_out[...] = along(0, channels) * scale
    at = channels + width
    grad_in[...] = along(channels, at) * scale
    bias_out[...] = (along(at, at + 128) + along(at + 128, at + 256)) * scale
    mixed = along(at + 256, at + 384) * scale
    loss[...] = -(mixed[2:3, 0:1] + mixed[3:4, 0:1])
    share = bias_in.shape[1]
    back = lax.rem(128 - lax.axis_index(Z) * share, 128)
    both = jnp.broadcast_to(mixed[0:1] + mixed[1:2], (ROWS, 128))
    bias_in[...] = pltpu.roll(both, back, 1)[0:1, :share]


def turn_kernel(dpre_t, dpre_pt, dpre, dpre_p):
    turn(dpre_pt, dpre_p)
    turn(dpre_t, dpre)


def hidden_kernel(dpre, dpre_r, w, grad, w_mine, w_other, s0, s1):
    c = lax.axis_index(C)
    copies = [gather(w, w_mine, s0, c), gather(w, w_other, s1, 1 - c)]
    for copy in copies:
        copy.wait()

    def columns(at):
        grad[:, at] = (nn(dpre[...], w_mine[:, at]) + nn(dpre_r[...], w_other[:, at])).astype(bf16)

    whole = grad.shape[1] // 256

    @pl.loop(0, whole)
    def _(i):
        columns(pl.ds(pl.multiple_of(i * 256, 256), 256))

    if whole * 256 < grad.shape[1]:
        columns(slice(whole * 256, grad.shape[1]))


def on_device(hidden_states, teacher, proj_in, bias_in, proj_out, bias_out):
    samples, seq, width = hidden_states.shape
    units, channels = proj_out.shape
    ny, nx, nc, nz = (lax.axis_size(a) for a in DP_FEAT)
    tokens = samples * seq
    block = units // (ny * nx * nc)
    half = units // nc
    share = block // nz
    scale = 1.0 / float(tokens * ny * nx * nc * nz)
    sems = pltpu.SemaphoreType.DMA
    one = 2 * half * tokens * channels

    rows = hidden_states.reshape(tokens, width)
    rows_p = shift(rows, C, 1)

    channel_rows = in_hbm(teacher.reshape(nz * tokens, channels // nz))
    pieces = [channel_rows] + [None] * (nz - 1)
    parts = call(
        functools.partial(split_kernel, TEACH),
        [HBM],
        [((tokens, channels // nz), bf16)] * len(TEACH),
        [pltpu.SemaphoreType.DMA((len(TEACH),))],
        limit=4,
    )(channel_rows)
    for k, part in zip(TEACH, parts):
        pieces[k] = shift(part, Z, k)

    w_in = in_hbm(proj_in.reshape(ny, nx, nc, block, width))
    w_out = in_hbm(proj_out.reshape(ny, nx, nc, block, channels))

    act_t, act_pt, slope, slope_p, act, act_p, out_mine, out_other = call(
        first_kernel,
        [VMEM, VMEM, HBM, HBM, VMEM],
        [((half, tokens), bf16)] * 2
        + [((half, tokens), f32)] * 2
        + [((tokens, half), bf16)] * 2
        + [((half, channels), bf16)] * 2,
        [pltpu.VMEM((half, width), bf16), pltpu.VMEM((half, 1), f32), sems, sems, sems],
        2 * one,
        12,
    )(rows, rows_p, w_in, w_out, bias_in[:, None])
    act_r = shift(act_p, C, 1)
    big = ((tokens, channels), f32)
    (out,) = call(out_kernel, [VMEM] * 3, [big], (), one)(act, out_mine, bias_out[None])
    (out,) = call(out_more_kernel, [VMEM] * 3, [big], (), one)(act_r, out_other, out)

    (cot,) = call(
        cot_kernel,
        [VMEM] + [HBM] * nz,
        [((tokens + ROWS, channels), bf16)],
        [
            pltpu.VMEM((8, 128), f32),
            pltpu.VMEM((2, nz, tokens // 2, channels // nz), bf16),
            pltpu.SemaphoreType.DMA((2,)),
        ],
        one // 4,
    )(out, channel_rows, *map(in_hbm, pieces[1:]))
    cot_p = shift(cot, C, 1)
    (dpre_t,) = call(back_kernel, [VMEM] * 3, [((half, tokens), bf16)], (), one)(
        cot, out_mine, slope
    )

    def messages(height, wide):
        return [((height + ROWS, wide), bf16)] * 3 + [((height, wide), f32)]

    quarter = RING * block
    inputs = (cot_p, out_mine, slope_p, dpre_t, rows, rows_p)
    (far,) = call(
        grad_in_far_kernel,
        [VMEM] * 6,
        messages(quarter, width)[:1],
        [pltpu.VMEM((quarter, tokens), bf16)] * 2,
        one,
    )(*inputs)
    *near, first_own, first_small, dpre_pt = call(
        grad_in_kernel,
        [VMEM] * 6,
        messages(quarter, width)[1:] + [((ROWS, 128), f32), ((half, tokens), bf16)],
        (),
        3 * one,
    )(*inputs)
    first = shifts((far, *near), Y)

    inputs = (act_t, act_pt, cot, cot_p)
    far, packed, last_small = call(
        grad_out_far_kernel,
        [VMEM] * 4,
        messages(quarter, channels)[:1] + [((ROWS, channels), bf16), ((ROWS, 256), f32)],
        (),
        one // 2,
    )(*inputs)
    *near, last_own = call(
        grad_out_kernel, [VMEM] * 5, messages(quarter, channels)[1:], (), 2 * one
    )(*inputs, packed)
    last = shifts((far, *near), X)

    dpre, dpre_p = call(
        turn_kernel, [VMEM] * 2, [((tokens, half), bf16)] * 2, (), one
    )(dpre_t, dpre_pt)
    dpre_r = shift(dpre_p, C, 1)

    *first, first_own, first_small = call(
        functools.partial(middle_kernel, True),
        [VMEM] * 5,
        messages(block, width) + [((ROWS, 128), f32)],
        (),
        one // 8,
    )(first_own, first_small, *first)
    first = shifts(first, X)
    *last, last_own, last_small = call(
        functools.partial(middle_kernel, False),
        [VMEM] * 5,
        messages(block, channels) + [((ROWS, 256), f32)],
        (),
        one // 8,
    )(last_own, last_small, *last)
    last = shifts(last, Y)

    (joint,) = call(
        joint_kernel, [VMEM] * 10, [((nz, share, channels + width + 384), bf16)], (), one // 8
    )(last_own, last_small, *last, first_own, first_small, *first)
    dpre_r, joint = lax.optimization_barrier((dpre_r, joint))
    joint = lax.all_to_all(joint, Z, split_axis=0, concat_axis=0, tiled=True)
    (grad_hidden,) = call(
        hidden_kernel,
        [VMEM, VMEM, HBM],
        [((tokens, width), bf16)],
        [pltpu.VMEM((half, width), bf16)] * 2 + [sems, sems],
        2 * one,
        20,
    )(dpre, dpre_r, w_in)
    grad_in, grad_out, grad_bias_out, loss, grad_bias_in = call(
        functools.partial(last_kernel, scale, width, channels),
        [VMEM],
        [((share, width), f32), ((share, channels), f32), ((ROWS, 128), f32)]
        + [((1, 1), f32), ((1, share), f32)],
    )(joint)
    return (
        grad_in,
        grad_bias_in.reshape(share),
        grad_out,
        grad_bias_out.reshape(channels),
        grad_hidden.reshape(samples, seq, width),
        loss.reshape(()),
    )


def solution(mesh):
    finer = Mesh(mesh.devices.reshape(4, 4, 2, mesh.shape["feat"]), DP_FEAT)
    return jax.shard_map(
        on_device,
        mesh=finer,
        in_specs=(P(DP_FEAT, None, None), P(DP, None, Z), P(), P(), P(), P()),
        out_specs=(
            P(DP_FEAT, None),
            P(DP_FEAT),
            P(DP_FEAT, None),
            P(),
            P(DP_FEAT, None, None),
            P(),
        ),
        check_vma=False,
    )
```

time: 150 us -> 135 us (0.900)
  local copies, waits for them, and re-layouts: 19 us -> 3.01 us
  starting transfers between devices: 41.1 us -> 48.6 us
  waiting for transfers between devices: 48.4 us -> 43.5 us
    unnamed x46 -> x20, local copies, waits for them, and re-layouts: 15.4 us -> 1.95 us
    ppermute x23, starting transfers between devices: 36.3 us -> 43.7 us  [shift(): return lax.ppermute(x, axis, [(i, (i + k) % n) for i in range(n)])]
    pallas_call x5 -> x8, Pallas kernels: 16.9 us -> 23.9 us  [the longest x1 7.04 us: on_device(): call(hidden_kernel, [VMEM, VMEM, HBM], [((tokens, width), bf16)], [pltpu....]
    pallas_call x1, Pallas kernels: 13.7 us -> 7.4 us  [on_device(): call(first_kernel, [VMEM, VMEM, HBM, HBM, VMEM], [((half, tokens), bf16)]...]
    ppermute x23, waiting for transfers between devices: 44.5 us -> 38.3 us  [shift(): return lax.ppermute(x, axis, [(i, (i + k) % n) for i in range(n)])]
    dynamic_slice x2 -> x0, local copies, waits for them, and re-layouts: 2.03 us -> none  [the longest x1 1.45 us: on_device(): piece = lax.dynamic_slice_in_dim(teacher, to * samples, samples, 0)]
    pallas_call x1, Pallas kernels: 2.67 us -> 0.74 us  [on_device(): call(turn_kernel, [VMEM] * 2, [((tokens, half), bf16)] * 2, (), one)]
  transfers between devices with their start and end apart: 24 -> 24, of which waited for: 15 -> 16; matrix products, arithmetic and copies ran while one was open for 2% -> 1% of each run, Pallas kernels for 13% -> 17%
where the time goes in v2:
time: 135 us; the launch traced here: 134 us
  starting transfers between devices  48.6 us (36%)
  waiting for transfers between devices  43.5 us (32%)
  Pallas kernels  38.3 us (28%)
  local copies, waits for them, and re-layouts  3.01 us (2%)
    ppermute x23, starting transfers between devices, shift(): return lax.ppermute(x, axis, [(i, (i + k) % n) for i in range(n)])  43.7 us
    ppermute x23, waiting for transfers between devices, shift(): return lax.ppermute(x, axis, [(i, (i + k) % n) for i in range(n)])  38.3 us
    pallas_call x1, Pallas kernels, on_device(): call(first_kernel, [VMEM, VMEM, HBM, HBM, VMEM], [((half, tokens), bf16)]...  7.4 us
    pallas_call x1, Pallas kernels, on_device(): call(hidden_kernel, [VMEM, VMEM, HBM], [((tokens, width), bf16)], [pltpu....  7.04 us
    all_to_all x1, waiting for transfers between devices, on_device(): joint = lax.all_to_all(joint, Z, split_axis=0, concat_axis=0, tiled=True)  5.2 us
    pallas_call x1, Pallas kernels, on_device(): call(grad_in_kernel, [VMEM] * 6, messages(quarter, width)[1:] + [((ROWS,...  5.08 us
    all_to_all x1, starting transfers between devices, on_device(): joint = lax.all_to_all(joint, Z, split_axis=0, concat_axis=0, tiled=True)  4.86 us
    pallas_call x1, Pallas kernels, on_device(): call(cot_kernel, [VMEM] + [HBM] * nz, [((tokens + ROWS, channels), bf16)]...  3.49 us
  transfers between devices with their start and end apart: 24, of which 16 were waited for; matrix products, arithmetic and copies ran while one was open for 1% of the time, Pallas kernels for 17%

profile of v2, /device:TPU:6, one launch (start us, length us, event | category | flops | bytes accessed | tf_op | source)
XLA Modules:
  0.0 134.2 jit_solution(9974777140972551810)
XLA Ops:
  5.1 7.4 %shard_map.109 = (bf16[1024,512]{1,0:T(8,128)(2,1)S(1)}, bf16[1024,512]{1,0:T(8,128)(2,1)S(1)}, f32[1024,512]{1,0:T(8,128)S(1)}, f32[1024,512]{1,0:T(8,128)S(1)}...) custom-call(bf16[512,1152]{1,0:T(8,128)(2,1)S(1)} %bitcast.11, ...), custom_call_target="tpu_custom_call" | custom-call | flops 2147483648 | bytes 4194304 | tf_op jit(solution)/shard_map/pallas_call | solution.py:469
  16.0 3.3 %collective-permute-start.3 = (bf16[512,128]{1,0:T(8,128)(2,1)S(1)}, bf16[512,128]{1,0:T(8,128)(2,1)S(1)}, u32[]{:S(2)}, u32[]{:S(2)}) collective-permute-start(bf16[512,128]{1,0:T(8,128)(2,1)S(1)} %get-tuple-element.56), channel_id=1, source_target_pairs={{0,2},{1,3},{2,4},{3,5},{4,6},{5,7},{6,0},{7,1},{8,10},{9,11},{10,... | collective-permute-start | bytes 393224 | tf_op jit(solution)/shard_map/ppermute | solution.py:30
  19.2 4.0 %collective-permute-start.4 = (bf16[512,128]{1,0:T(8,128)(2,1)S(1)}, bf16[512,128]{1,0:T(8,128)(2,1)S(1)}, u32[]{:S(2)}, u32[]{:S(2)}) collective-permute-start(bf16[512,128]{1,0:T(8,128)(2,1)S(1)} %get-tuple-element.57), channel_id=1, source_target_pairs={{0,3},{1,4},{2,5},{3,6},{4,7},{5,0},{6,1},{7,2},{8,11},{9,12},{10,... | collective-permute-start | bytes 393224 | tf_op jit(solution)/shard_map/ppermute | solution.py:30
  24.3 4.5 %collective-permute-start.6 = (bf16[512,128]{1,0:T(8,128)(2,1)S(1)}, bf16[512,128]{1,0:T(8,128)(2,1)S(1)}, u32[]{:S(2)}, u32[]{:S(2)}) collective-permute-start(bf16[512,128]{1,0:T(8,128)(2,1)S(1)} %get-tuple-element.59), channel_id=1, source_target_pairs={{0,5},{1,6},{2,7},{3,0},{4,1},{5,2},{6,3},{7,4},{8,13},{9,14},{10,... | collective-permute-start | bytes 393224 | tf_op jit(solution)/shard_map/ppermute | solution.py:30
  28.8 3.4 %collective-permute-done.3.refs_2_ = bf16[512,128]{1,0:T(8,128)(2,1)S(1)} collective-permute-done((bf16[512,128]{1,0:T(8,128)(2,1)S(1)}, bf16[512,128]{1,0:T(8,128)(2,1)S(1)}, u32[]{:S(2)}, u32[]{:S(2)}) %collective-permute-start.3) | collective-permute-done | bytes 131104 | tf_op jit(solution)/shard_map/ppermute | solution.py:30
  37.9 3.4 %collective-permute-done.4.refs_3_ = bf16[512,128]{1,0:T(8,128)(2,1)S(1)} collective-permute-done((bf16[512,128]{1,0:T(8,128)(2,1)S(1)}, bf16[512,128]{1,0:T(8,128)(2,1)S(1)}, u32[]{:S(2)}, u32[]{:S(2)}) %collective-permute-start.4) | collective-permute-done | bytes 131104 | tf_op jit(solution)/shard_map/ppermute | solution.py:30
  41.3 3.0 %collective-permute-done.6.refs_5_ = bf16[512,128]{1,0:T(8,128)(2,1)S(1)} collective-permute-done((bf16[512,128]{1,0:T(8,128)(2,1)S(1)}, bf16[512,128]{1,0:T(8,128)(2,1)S(1)}, u32[]{:S(2)}, u32[]{:S(2)}) %collective-permute-start.6) | collective-permute-done | bytes 131104 | tf_op jit(solution)/shard_map/ppermute | solution.py:30
  44.3 3.9 %collective-permute-done.7.refs_6_ = bf16[512,128]{1,0:T(8,128)(2,1)S(1)} collective-permute-done((bf16[512,128]{1,0:T(8,128)(2,1)S(1)}, bf16[512,128]{1,0:T(8,128)(2,1)S(1)}, u32[]{:S(2)}, u32[]{:S(2)}) %collective-permute-start.7) | collective-permute-done | bytes 131104 | tf_op jit(solution)/shard_map/ppermute | solution.py:30
  49.7 3.5 %shard_map.113.cot = bf16[520,1024]{1,0:T(8,128)(2,1)S(1)} custom-call(f32[512,1024]{1,0:T(8,128)S(1)} %shard_map.111.out, bf16[4096,128]{1,0:T(8,128)(2,1)} %bitcast.19, bf16[512,128]{1,0:T(8,128)(2,1)} %copy-done.3, bf16[512,128]{1,0:T(8,128)(2,1)} %copy-done.4, bf16[512,128]{1,0:T(8,128)(2,1)} %copy-done.5, bf16[512,128]{1,0:T(8,128)(2,1)} %copy-done.6, ...), custom_call_target="tpu_custom_call" | custom-call | flops 268435456 | bytes 4194304 | tf_op jit(solution)/shard_map/pallas_call | solution.py:485
  57.6 2.3 %shard_map.118 = (bf16[264,1024]{1,0:T(8,128)(2,1)S(1)}, bf16[264,1024]{1,0:T(8,128)(2,1)S(1)}, f32[256,1024]{1,0:T(8,128)S(1)}) custom-call(bf16[1024,512]{1,0:T(8,128)(2,1)S(1)} %get-tuple-element.66.act, bf16[1024,512]{1,0:T(8,128)(2,1)S(1)} %get-tuple-element.67.act_p, bf16[520,1024]{1,0:T(8,128)(2,1)S(1)} %shard_map.113.cot, ...), custom_call_target="tpu_custom_call" | custom-call | flops 2147483648 | bytes 4194304 | tf_op jit(solution)/shard_map/pallas_call | solution.py:530
  61.1 2.4 %collective-permute-start.13 = (bf16[264,1024]{1,0:T(8,128)(2,1)S(1)}, bf16[264,1024]{1,0:T(8,128)(2,1)S(1)}, u32[]{:S(2)}, u32[]{:S(2)}) collective-permute-start(bf16[264,1024]{1,0:T(8,128)(2,1)S(1)} %get-tuple-element.73), channel_id=1, source_target_pairs={{0,16},{16,32},{32,48},{48,0},{1,17},{17,33},{33,49},{49,1},{2,18}... | collective-permute-start | bytes 1622024 | tf_op jit(solution)/shard_map/ppermute | solution.py:30
  63.5 5.1 %shard_map.115 = (bf16[264,1152]{1,0:T(8,128)(2,1)S(1)}, bf16[264,1152]{1,0:T(8,128)(2,1)S(1)}, f32[256,1152]{1,0:T(8,128)S(1)}, f32[8,128]{1,0:T(8,128)S(1)}, bf16[1024,512]{1,0:T(8,128)(2,1)S(1)}) custom-call(bf16[520,1024]{1,0:T(8,128)(2,1)S(1)} %collective-permute-done.9.cot_p, bf16[1024,1024]{1,0:T(8,128)(2,1)S(1)} %get-tuple-element.54.w.w_mine, ...), custom_call_target="tpu_custom_call" | custom-call | flops 3221225472 | bytes 4194304 | tf_op jit(solution)/shard_map/pallas_call | solution.py:513
  69.4 2.0 %shard_map.120 = bf16[264,1152]{1,0:T(8,128)(2,1)S(1)} custom-call(bf16[520,1024]{1,0:T(8,128)(2,1)S(1)} %collective-permute-done.9.cot_p, bf16[1024,1024]{1,0:T(8,128)(2,1)S(1)} %get-tuple-element.54.w.w_mine, f32[1024,512]{1,0:T(8,128)S(1)} %get-tuple-element.63.slope_p, bf16[1024,512]{1,0:T(8,128)(2,1)S(1)} %shard_map.114.dpre.dpre_t, ...), custom_call_target="tpu_custom_call" | custom-call | flops 1073741824 | bytes 4194304 | tf_op jit(solution)/shard_map/pallas_call | solution.py:506
  71.5 3.3 %collective-permute-start.17 = (bf16[264,1152]{1,0:T(8,128)(2,1)S(1)}, bf16[264,1152]{1,0:T(8,128)(2,1)S(1)}, u32[]{:S(2)}, u32[]{:S(2)}) collective-permute-start(bf16[264,1152]{1,0:T(8,128)(2,1)S(1)} %shard_map.120), channel_id=1, source_target_pairs={{0,128},{64,192},{128,0},{192,64},{1,129},{65,193},{129,1},{193,65... | collective-permute-start | bytes 1824776 | tf_op jit(solution)/shard_map/ppermute | solution.py:30
  75.8 3.0 %collective-permute-start.18 = (bf16[264,1152]{1,0:T(8,128)(2,1)S(1)}, bf16[264,1152]{1,0:T(8,128)(2,1)S(1)}, u32[]{:S(2)}, u32[]{:S(2)}) collective-permute-start(bf16[264,1152]{1,0:T(8,128)(2,1)S(1)} %get-tuple-element.81), channel_id=1, source_target_pairs={{0,192},{64,0},{128,64},{192,128},{1,193},{65,1},{129,65},{193,129... | collective-permute-start | bytes 1824776 | tf_op jit(solution)/shard_map/ppermute | solution.py:30
  78.8 9.4 %collective-permute-start.19 = (bf16[264,1152]{1,0:T(8,128)(2,1)S(1)}, bf16[264,1152]{1,0:T(8,128)(2,1)S(1)}, u32[]{:S(2)}, u32[]{:S(2)}) collective-permute-start(bf16[264,1152]{1,0:T(8,128)(2,1)S(1)} %get-tuple-element.82), channel_id=1, source_target_pairs={{0,64},{64,128},{128,192},{192,0},{1,65},{65,129},{129,193},{193,1... | collective-permute-start | bytes 1824776 | tf_op jit(solution)/shard_map/ppermute | solution.py:30
  88.2 2.5 %collective-permute-done.11.g_a = bf16[264,1024]{1,0:T(8,128)(2,1)S(1)} collective-permute-done((bf16[264,1024]{1,0:T(8,128)(2,1)S(1)}, bf16[264,1024]{1,0:T(8,128)(2,1)S(1)}, u32[]{:S(2)}, u32[]{:S(2)}) %collective-permute-start.11) | collective-permute-done | bytes 540704 | tf_op jit(solution)/shard_map/ppermute | solution.py:30
  91.5 2.9 %collective-permute-start.15 = (bf16[72,1024]{1,0:T(8,128)(2,1)S(1)}, bf16[72,1024]{1,0:T(8,128)(2,1)S(1)}, u32[]{:S(2)}, u32[]{:S(2)}) collective-permute-start(bf16[72,1024]{1,0:T(8,128)(2,1)S(1)} %get-tuple-element.77), channel_id=1, source_target_pairs={{0,192},{64,0},{128,64},{192,128},{1,193},{65,1},{129,65},{193,129... | collective-permute-start | bytes 442376 | tf_op jit(solution)/shard_map/ppermute | solution.py:30
  94.3 8.7 %collective-permute-done.18.g_b = bf16[264,1152]{1,0:T(8,128)(2,1)S(1)} collective-permute-done((bf16[264,1152]{1,0:T(8,128)(2,1)S(1)}, bf16[264,1152]{1,0:T(8,128)(2,1)S(1)}, u32[]{:S(2)}, u32[]{:S(2)}) %collective-permute-start.18) | collective-permute-done | bytes 608288 | tf_op jit(solution)/shard_map/ppermute | solution.py:30
  105.4 2.1 %collective-permute-start.22 = (bf16[72,1152]{1,0:T(8,128)(2,1)S(1)}, bf16[72,1152]{1,0:T(8,128)(2,1)S(1)}, u32[]{:S(2)}, u32[]{:S(2)}) collective-permute-start(bf16[72,1152]{1,0:T(8,128)(2,1)S(1)} %get-tuple-element.87), channel_id=1, source_target_pairs={{0,16},{16,32},{32,48},{48,0},{1,17},{17,33},{33,49},{49,1},{2,18}... | collective-permute-start | bytes 497672 | tf_op jit(solution)/shard_map/ppermute | solution.py:30
  110.0 5.5 %collective-permute-done.16.o3 = bf16[72,1024]{1,0:T(8,128)(2,1)S(1)} collective-permute-done((bf16[72,1024]{1,0:T(8,128)(2,1)S(1)}, bf16[72,1024]{1,0:T(8,128)(2,1)S(1)}, u32[]{:S(2)}, u32[]{:S(2)}) %collective-permute-start.16) | collective-permute-done | bytes 147488 | tf_op jit(solution)/shard_map/ppermute | solution.py:30
  116.5 4.9 %all-to-all-start = ((bf16[8,8,2560]{2,1,0:T(8,128)(2,1)}), bf16[8,8,2560]{2,1,0:T(8,128)(2,1)S(1)}, u32[]{:S(2)}, u32[]{:S(2)}) async-start(bf16[8,8,2560]{2,1,0:T(8,128)(2,1)} %shard_map.122), calls=%async_computation | async-start | bytes 655360 | tf_op jit(solution)/shard_map/all_to_all | solution.py:561
  121.3 7.0 %shard_map.124 = bf16[512,1152]{1,0:T(8,128)(2,1)} custom-call(bf16[512,1024]{1,0:T(8,128)(2,1)S(1)} %get-tuple-element.93.dpre, bf16[512,1024]{1,0:T(8,128)(2,1)S(1)} %collective-permute-done.10.dpre_r, bf16[4,4,2,64,1152]{4,3,2,1,0:T(8,128)(2,1)} %bitcast.16), custom_call_target="tpu_custom_call" | custom-call | flops 2147483648 | bytes 4194304 | tf_op jit(solution)/shard_map/pallas_call | solution.py:562
  128.4 5.2 %all-to-all-done.joint = bf16[8,8,2560]{2,1,0:T(8,128)(2,1)S(1)} async-done(((bf16[8,8,2560]{2,1,0:T(8,128)(2,1)}), bf16[8,8,2560]{2,1,0:T(8,128)(2,1)S(1)}, u32[]{:S(2)}, u32[]{:S(2)}) %all-to-all-start) | async-done | bytes 327712 | tf_op jit(solution)/shard_map/all_to_all | solution.py:561
  (61 shorter events, 30.7 us)
Async XLA Ops:
  0.6 3.1 %collective-permute-start = (bf16[512,1152]{1,0:T(8,128)(2,1)}, bf16[512,1152]{1,0:T(8,128)(2,1)S(1)}, u32[]{:S(2)}, u32[]{:S(2)}) collective-permute-start(bf16[512,1152]{1,0:T(8,128)(2,1)} %bitcast.10), channel_id=1, source_target_pairs={{0,8},{8,0},{1,9},{9,1},{2,10},{10,2},{3,11},{11,3},{4,12},{12,4},... | collective-permute-start | bytes 3538952 | tf_op jit(solution)/shard_map/ppermute | solution.py:30
  12.5 19.8 %collective-permute-start.1 = (bf16[512,1024]{1,0:T(8,128)(2,1)S(1)}, bf16[512,1024]{1,0:T(8,128)(2,1)S(1)}, u32[]{:S(2)}, u32[]{:S(2)}) collective-permute-start(bf16[512,1024]{1,0:T(8,128)(2,1)S(1)} %get-tuple-element.51), channel_id=1, source_target_pairs={{0,8},{8,0},{1,9},{9,1},{2,10},{10,2},{3,11},{11,3},{4,12},{12,4},... | collective-permute-start | bytes 3145736 | tf_op jit(solution)/shard_map/ppermute | solution.py:30
  14.0 10.3 %collective-permute-start.2 = (bf16[512,128]{1,0:T(8,128)(2,1)S(1)}, bf16[512,128]{1,0:T(8,128)(2,1)S(1)}, u32[]{:S(2)}, u32[]{:S(2)}) collective-permute-start(bf16[512,128]{1,0:T(8,128)(2,1)S(1)} %get-tuple-element.55), channel_id=1, source_target_pairs={{0,1},{1,2},{2,3},{3,4},{4,5},{5,6},{6,7},{7,0},{8,9},{9,10},{10,1... | collective-permute-start | bytes 393224 | tf_op jit(solution)/shard_map/ppermute | solution.py:30
  16.0 16.2 %collective-permute-start.3 = (bf16[512,128]{1,0:T(8,128)(2,1)S(1)}, bf16[512,128]{1,0:T(8,128)(2,1)S(1)}, u32[]{:S(2)}, u32[]{:S(2)}) collective-permute-start(bf16[512,128]{1,0:T(8,128)(2,1)S(1)} %get-tuple-element.56), channel_id=1, source_target_pairs={{0,2},{1,3},{2,4},{3,5},{4,6},{5,7},{6,0},{7,1},{8,10},{9,11},{10,... | collective-permute-start | bytes 393224 | tf_op jit(solution)/shard_map/ppermute | solution.py:30
  19.2 22.0 %collective-permute-start.4 = (bf16[512,128]{1,0:T(8,128)(2,1)S(1)}, bf16[512,128]{1,0:T(8,128)(2,1)S(1)}, u32[]{:S(2)}, u32[]{:S(2)}) collective-permute-start(bf16[512,128]{1,0:T(8,128)(2,1)S(1)} %get-tuple-element.57), channel_id=1, source_target_pairs={{0,3},{1,4},{2,5},{3,6},{4,7},{5,0},{6,1},{7,2},{8,11},{9,12},{10,... | collective-permute-start | bytes 393224 | tf_op jit(solution)/shard_map/ppermute | solution.py:30
  23.3 18.0 %collective-permute-start.5 = (bf16[512,128]{1,0:T(8,128)(2,1)S(1)}, bf16[512,128]{1,0:T(8,128)(2,1)S(1)}, u32[]{:S(2)}, u32[]{:S(2)}) collective-permute-start(bf16[512,128]{1,0:T(8,128)(2,1)S(1)} %get-tuple-element.58), channel_id=1, source_target_pairs={{0,4},{1,5},{2,6},{3,7},{4,0},{5,1},{6,2},{7,3},{8,12},{9,13},{10,... | collective-permute-start | bytes 393224 | tf_op jit(solution)/shard_map/ppermute | solution.py:30
  24.3 20.0 %collective-permute-start.6 = (bf16[512,128]{1,0:T(8,128)(2,1)S(1)}, bf16[512,128]{1,0:T(8,128)(2,1)S(1)}, u32[]{:S(2)}, u32[]{:S(2)}) collective-permute-start(bf16[512,128]{1,0:T(8,128)(2,1)S(1)} %get-tuple-element.59), channel_id=1, source_target_pairs={{0,5},{1,6},{2,7},{3,0},{4,1},{5,2},{6,3},{7,4},{8,13},{9,14},{10,... | collective-permute-start | bytes 393224 | tf_op jit(solution)/shard_map/ppermute | solution.py:30
  32.2 15.9 %collective-permute-start.7 = (bf16[512,128]{1,0:T(8,128)(2,1)S(1)}, bf16[512,128]{1,0:T(8,128)(2,1)S(1)}, u32[]{:S(2)}, u32[]{:S(2)}) collective-permute-start(bf16[512,128]{1,0:T(8,128)(2,1)S(1)} %get-tuple-element.60), channel_id=1, source_target_pairs={{0,6},{1,7},{2,0},{3,1},{4,2},{5,3},{6,4},{7,5},{8,14},{9,15},{10,... | collective-permute-start | bytes 393224 | tf_op jit(solution)/shard_map/ppermute | solution.py:30
  32.2 16.8 %collective-permute-start.8 = (bf16[512,128]{1,0:T(8,128)(2,1)S(1)}, bf16[512,128]{1,0:T(8,128)(2,1)S(1)}, u32[]{:S(2)}, u32[]{:S(2)}) collective-permute-start(bf16[512,128]{1,0:T(8,128)(2,1)S(1)} %get-tuple-element.61), channel_id=1, source_target_pairs={{0,7},{1,0},{2,1},{3,2},{4,3},{5,4},{6,5},{7,6},{8,15},{9,8},{10,9... | collective-permute-start | bytes 393224 | tf_op jit(solution)/shard_map/ppermute | solution.py:30
  53.2 2.8 %collective-permute-start.9 = (bf16[520,1024]{1,0:T(8,128)(2,1)S(1)}, bf16[520,1024]{1,0:T(8,128)(2,1)S(1)}, u32[]{:S(2)}, u32[]{:S(2)}) collective-permute-start(bf16[520,1024]{1,0:T(8,128)(2,1)S(1)} %shard_map.113.cot), channel_id=1, source_target_pairs={{0,8},{8,0},{1,9},{9,1},{2,10},{10,2},{3,11},{11,3},{4,12},{12,4},... | collective-permute-start | bytes 3194888 | tf_op jit(solution)/shard_map/ppermute | solution.py:30
  60.0 15.8 %collective-permute-start.12 = (bf16[264,1024]{1,0:T(8,128)(2,1)S(1)}, bf16[264,1024]{1,0:T(8,128)(2,1)S(1)}, u32[]{:S(2)}, u32[]{:S(2)}) collective-permute-start(bf16[264,1024]{1,0:T(8,128)(2,1)S(1)} %get-tuple-element.72), channel_id=1, source_target_pairs={{0,48},{16,0},{32,16},{48,32},{1,49},{17,1},{33,17},{49,33},{2,50}... | collective-permute-start | bytes 1622024 | tf_op jit(solution)/shard_map/ppermute | solution.py:30
  61.1 17.7 %collective-permute-start.13 = (bf16[264,1024]{1,0:T(8,128)(2,1)S(1)}, bf16[264,1024]{1,0:T(8,128)(2,1)S(1)}, u32[]{:S(2)}, u32[]{:S(2)}) collective-permute-start(bf16[264,1024]{1,0:T(8,128)(2,1)S(1)} %get-tuple-element.73), channel_id=1, source_target_pairs={{0,16},{16,32},{32,48},{48,0},{1,17},{17,33},{33,49},{49,1},{2,18}... | collective-permute-start | bytes 1622024 | tf_op jit(solution)/shard_map/ppermute | solution.py:30
  69.3 47.2 %collective-permute-start.10 = (bf16[512,1024]{1,0:T(8,128)(2,1)S(1)}, bf16[512,1024]{1,0:T(8,128)(2,1)S(1)}, u32[]{:S(2)}, u32[]{:S(2)}) collective-permute-start(bf16[512,1024]{1,0:T(8,128)(2,1)S(1)} %get-tuple-element.65), channel_id=1, source_target_pairs={{0,8},{8,0},{1,9},{9,1},{2,10},{10,2},{3,11},{11,3},{4,12},{12,4},... | collective-permute-start | bytes 3145736 | tf_op jit(solution)/shard_map/ppermute | solution.py:30
  71.5 20.0 %collective-permute-start.17 = (bf16[264,1152]{1,0:T(8,128)(2,1)S(1)}, bf16[264,1152]{1,0:T(8,128)(2,1)S(1)}, u32[]{:S(2)}, u32[]{:S(2)}) collective-permute-start(bf16[264,1152]{1,0:T(8,128)(2,1)S(1)} %shard_map.120), channel_id=1, source_target_pairs={{0,128},{64,192},{128,0},{192,64},{1,129},{65,193},{129,1},{193,65... | collective-permute-start | bytes 1824776 | tf_op jit(solution)/shard_map/ppermute | solution.py:30
  74.7 15.9 %collective-permute-start.11 = (bf16[264,1024]{1,0:T(8,128)(2,1)S(1)}, bf16[264,1024]{1,0:T(8,128)(2,1)S(1)}, u32[]{:S(2)}, u32[]{:S(2)}) collective-permute-start(bf16[264,1024]{1,0:T(8,128)(2,1)S(1)} %get-tuple-element.71), channel_id=1, source_target_pairs={{0,32},{16,48},{32,0},{48,16},{1,33},{17,49},{33,1},{49,17},{2,34}... | collective-permute-start | bytes 1622024 | tf_op jit(solution)/shard_map/ppermute | solution.py:30
  75.8 27.3 %collective-permute-start.18 = (bf16[264,1152]{1,0:T(8,128)(2,1)S(1)}, bf16[264,1152]{1,0:T(8,128)(2,1)S(1)}, u32[]{:S(2)}, u32[]{:S(2)}) collective-permute-start(bf16[264,1152]{1,0:T(8,128)(2,1)S(1)} %get-tuple-element.81), channel_id=1, source_target_pairs={{0,192},{64,0},{128,64},{192,128},{1,193},{65,1},{129,65},{193,129... | collective-permute-start | bytes 1824776 | tf_op jit(solution)/shard_map/ppermute | solution.py:30
  78.8 25.0 %collective-permute-start.19 = (bf16[264,1152]{1,0:T(8,128)(2,1)S(1)}, bf16[264,1152]{1,0:T(8,128)(2,1)S(1)}, u32[]{:S(2)}, u32[]{:S(2)}) collective-permute-start(bf16[264,1152]{1,0:T(8,128)(2,1)S(1)} %get-tuple-element.82), channel_id=1, source_target_pairs={{0,64},{64,128},{128,192},{192,0},{1,65},{65,129},{129,193},{193,1... | collective-permute-start | bytes 1824776 | tf_op jit(solution)/shard_map/ppermute | solution.py:30
  90.9 14.5 %collective-permute-start.14 = (bf16[72,1024]{1,0:T(8,128)(2,1)S(1)}, bf16[72,1024]{1,0:T(8,128)(2,1)S(1)}, u32[]{:S(2)}, u32[]{:S(2)}) collective-permute-start(bf16[72,1024]{1,0:T(8,128)(2,1)S(1)} %get-tuple-element.76), channel_id=1, source_target_pairs={{0,128},{64,192},{128,0},{192,64},{1,129},{65,193},{129,1},{193,65... | collective-permute-start | bytes 442376 | tf_op jit(solution)/shard_map/ppermute | solution.py:30
  91.5 17.5 %collective-permute-start.15 = (bf16[72,1024]{1,0:T(8,128)(2,1)S(1)}, bf16[72,1024]{1,0:T(8,128)(2,1)S(1)}, u32[]{:S(2)}, u32[]{:S(2)}) collective-permute-start(bf16[72,1024]{1,0:T(8,128)(2,1)S(1)} %get-tuple-element.77), channel_id=1, source_target_pairs={{0,192},{64,0},{128,64},{192,128},{1,193},{65,1},{129,65},{193,129... | collective-permute-start | bytes 442376 | tf_op jit(solution)/shard_map/ppermute | solution.py:30
  104.1 11.5 %collective-permute-start.20 = (bf16[72,1152]{1,0:T(8,128)(2,1)S(1)}, bf16[72,1152]{1,0:T(8,128)(2,1)S(1)}, u32[]{:S(2)}, u32[]{:S(2)}) collective-permute-start(bf16[72,1152]{1,0:T(8,128)(2,1)S(1)} %get-tuple-element.85), channel_id=1, source_target_pairs={{0,32},{16,48},{32,0},{48,16},{1,33},{17,49},{33,1},{49,17},{2,34}... | collective-permute-start | bytes 497672 | tf_op jit(solution)/shard_map/ppermute | solution.py:30
  104.2 11.4 %collective-permute-start.21 = (bf16[72,1152]{1,0:T(8,128)(2,1)S(1)}, bf16[72,1152]{1,0:T(8,128)(2,1)S(1)}, u32[]{:S(2)}, u32[]{:S(2)}) collective-permute-start(bf16[72,1152]{1,0:T(8,128)(2,1)S(1)} %get-tuple-element.86), channel_id=1, source_target_pairs={{0,48},{16,0},{32,16},{48,32},{1,49},{17,1},{33,17},{49,33},{2,50}... | collective-permute-start | bytes 497672 | tf_op jit(solution)/shard_map/ppermute | solution.py:30
  105.4 10.2 %collective-permute-start.22 = (bf16[72,1152]{1,0:T(8,128)(2,1)S(1)}, bf16[72,1152]{1,0:T(8,128)(2,1)S(1)}, u32[]{:S(2)}, u32[]{:S(2)}) collective-permute-start(bf16[72,1152]{1,0:T(8,128)(2,1)S(1)} %get-tuple-element.87), channel_id=1, source_target_pairs={{0,16},{16,32},{32,48},{48,0},{1,17},{17,33},{33,49},{49,1},{2,18}... | collective-permute-start | bytes 497672 | tf_op jit(solution)/shard_map/ppermute | solution.py:30
  109.0 6.6 %collective-permute-start.16 = (bf16[72,1024]{1,0:T(8,128)(2,1)S(1)}, bf16[72,1024]{1,0:T(8,128)(2,1)S(1)}, u32[]{:S(2)}, u32[]{:S(2)}) collective-permute-start(bf16[72,1024]{1,0:T(8,128)(2,1)S(1)} %get-tuple-element.78), channel_id=1, source_target_pairs={{0,64},{64,128},{128,192},{192,0},{1,65},{65,129},{129,193},{193,1... | collective-permute-start | bytes 442376 | tf_op jit(solution)/shard_map/ppermute | solution.py:30
  116.5 17.1 %all-to-all-start = ((bf16[8,8,2560]{2,1,0:T(8,128)(2,1)}), bf16[8,8,2560]{2,1,0:T(8,128)(2,1)S(1)}, u32[]{:S(2)}, u32[]{:S(2)}) async-start(bf16[8,8,2560]{2,1,0:T(8,128)(2,1)} %shard_map.122), calls=%async_computation | async-start | bytes 655360 | tf_op jit(solution)/shard_map/all_to_all | solution.py:561
  (10 other events, 73.6 us)

commit v3 on v2

--- a/solution.py
+++ b/solution.py
@@ -95,20 +95,28 @@
 
 
 def first_kernel(
-    rows, rows_p, w_in, w_out, bias, act_t, act_pt, slope, slope_p, act, act_p, out_mine,
-    out_other, in_mine, col, s0, s1, s2,
+    rows_hbm, rows_p, w_in, w_out, bias_hbm, act_t, act_pt, slope, slope_p, act, act_p, out_mine,
+    out_other, in_mine, rows, bias, col, s0, s1, s2, s3,
 ):
     y, x, c = lax.axis_index(Y), lax.axis_index(X), lax.axis_index(C)
+    bias_copy = pltpu.make_async_copy(bias_hbm, bias, s3.at[0])
+    rows_copy = pltpu.make_async_copy(rows_hbm, rows, s3.at[1])
+    bias_copy.start()
     now = gather(w_in, in_mine, s0, c)
+    rows_copy.start()
     later = [gather(w_out, out_mine, s1, c), gather(w_out, out_other, s2, 1 - c)]
     block = w_in.shape[3]
+    unit = lax.broadcasted_iota(jnp.int32, (block, bias.shape[1]), 0)
+    lane = lax.broadcasted_iota(jnp.int32, (block, bias.shape[1]), 1)
+    ours = lane == unit + c * block
+    bias_copy.wait()
     for kx in range(RING):
         for ky in range(RING):
-            of = (lax.rem(y + ky, RING) * RING + lax.rem(x + kx, RING)) * 2 + c
-            col[pl.ds((kx * RING + ky) * block, block), :] = bias[
-                pl.ds(pl.multiple_of(of * block, block), block), :
-            ]
+            of = lax.rem(y + ky, RING) * RING + lax.rem(x + kx, RING)
+            terms = jnp.where(ours, bias[pl.ds(of, 1), :], 0.0)
+            col[pl.ds((kx * RING + ky) * block, block), :] = jnp.sum(terms, axis=1, keepdims=True)
     now.wait()
+    rows_copy.wait()
 
     for r, a, s in ((rows, act_t, slope), (rows_p, act_pt, slope_p)):
 
@@ -155,45 +163,34 @@
 
 
 def cot_kernel(out, *refs):
-    given, (cot, total_ref, held, sems) = refs[:-4], refs[-4:]
+    pieces, (cot, total_ref) = refs[:-2], refs[-2:]
     z = lax.axis_index(Z)
-    n = len(given)
+    n = len(pieces)
     tokens = out.shape[0]
-    lanes = given[0].shape[1]
-    part = tokens // 2
-    for p in range(2):
-        for k, piece in enumerate(given):
-            rows = pl.ds(p * part, part)
-            if k == 0:
-                rows = pl.ds(pl.multiple_of(z * tokens + p * part, part), part)
-            pltpu.make_async_copy(piece.at[rows], held.at[p, k], sems.at[p]).start()
+    lanes = pieces[0].shape[1]
     total_ref[...] = jnp.zeros_like(total_ref)
     step = 64
 
     def of(k):
         return pl.ds(pl.multiple_of(lax.rem(z - k + n, n) * lanes, lanes), lanes)
 
-    for p in range(2):
-        pltpu.make_async_copy(held.at[p], held.at[p], sems.at[p]).wait()
-
-        @pl.loop(0, part // step)
-        def _(i):
-            of_part = pl.ds(pl.multiple_of(i * step, step), step)
-            at = pl.ds(pl.multiple_of(p * part + i * step, step), step)
-            zz = yy = zy = jnp.zeros((step, lanes), f32)
-            for k in range(n):
-                o, t = out[at, of(k)], held[p, k, of_part, :].astype(f32)
-                zz, yy, zy = zz + o * o, yy + t * t, zy + o * t
-            zz, yy, zy = (jnp.sum(v, axis=1, keepdims=True) for v in (zz, yy, zy))
-            norm_z = jnp.sqrt(zz + epsilon)
-            norms = norm_z * jnp.sqrt(yy + epsilon)
-            cosine = zy / norms
-            total_ref[...] += jnp.sum(cosine)
-            by_target = 1.0 / norms
-            by_out = cosine / (norm_z * norm_z)
-            for k in range(n):
-                o, t = out[at, of(k)], held[p, k, of_part, :].astype(f32)
-                cot[at, of(k)] = (by_out * o - t * by_target).astype(bf16)
+    @pl.loop(0, tokens // step)
+    def _(i):
+        at = pl.ds(pl.multiple_of(i * step, step), step)
+        zz = yy = zy = jnp.zeros((step, lanes), f32)
+        for k, piece in enumerate(pieces):
+            o, t = out[at, of(k)], piece[at, :].astype(f32)
+            zz, yy, zy = zz + o * o, yy + t * t, zy + o * t
+        zz, yy, zy = (jnp.sum(v, axis=1, keepdims=True) for v in (zz, yy, zy))
+        norm_z = jnp.sqrt(zz + epsilon)
+        norms = norm_z * jnp.sqrt(yy + epsilon)
+        cosine = zy / norms
+        total_ref[...] += jnp.sum(cosine)
+        by_target = 1.0 / norms
+        by_out = cosine / (norm_z * norm_z)
+        for k, piece in enumerate(pieces):
+            o, t = out[at, of(k)], piece[at, :].astype(f32)
+            cot[at, of(k)] = (by_out * o - t * by_target).astype(bf16)
 
     high, low = high_low(jnp.broadcast_to(total_ref[0:1, 0:1], (ROWS, cot.shape[1])))
     row = lax.broadcasted_iota(jnp.int32, high.shape, 0)
@@ -452,14 +449,14 @@
     rows_p = shift(rows, C, 1)
 
     channel_rows = in_hbm(teacher.reshape(nz * tokens, channels // nz))
-    pieces = [channel_rows] + [None] * (nz - 1)
     parts = call(
-        functools.partial(split_kernel, TEACH),
+        functools.partial(split_kernel, (*TEACH, 0)),
         [HBM],
-        [((tokens, channels // nz), bf16)] * len(TEACH),
-        [pltpu.SemaphoreType.DMA((len(TEACH),))],
+        [((tokens, channels // nz), bf16)] * nz,
+        [pltpu.SemaphoreType.DMA((nz,))],
         limit=4,
     )(channel_rows)
+    pieces = [parts[-1]] + [None] * (nz - 1)
     for k, part in zip(TEACH, parts):
         pieces[k] = shift(part, Z, k)
 
@@ -468,15 +465,24 @@
 
     act_t, act_pt, slope, slope_p, act, act_p, out_mine, out_other = call(
         first_kernel,
-        [VMEM, VMEM, HBM, HBM, VMEM],
+        [HBM, VMEM, HBM, HBM, HBM],
         [((half, tokens), bf16)] * 2
         + [((half, tokens), f32)] * 2
         + [((tokens, half), bf16)] * 2
         + [((half, channels), bf16)] * 2,
-        [pltpu.VMEM((half, width), bf16), pltpu.VMEM((half, 1), f32), sems, sems, sems],
+        [
+            pltpu.VMEM((half, width), bf16),
+            pltpu.VMEM((tokens, width), bf16),
+            pltpu.VMEM((ny * nx, nc * block), f32),
+            pltpu.VMEM((half, 1), f32),
+            sems,
+            sems,
+            sems,
+            pltpu.SemaphoreType.DMA((2,)),
+        ],
         2 * one,
         12,
-    )(rows, rows_p, w_in, w_out, bias_in[:, None])
+    )(in_hbm(rows), rows_p, w_in, w_out, in_hbm(bias_in.reshape(ny * nx, nc * block)))
     act_r = shift(act_p, C, 1)
     big = ((tokens, channels), f32)
     (out,) = call(out_kernel, [VMEM] * 3, [big], (), one)(act, out_mine, bias_out[None])
@@ -484,15 +490,11 @@
 
     (cot,) = call(
         cot_kernel,
-        [VMEM] + [HBM] * nz,
+        [VMEM] * (1 + nz),
         [((tokens + ROWS, channels), bf16)],
-        [
-            pltpu.VMEM((8, 128), f32),
-            pltpu.VMEM((2, nz, tokens // 2, channels // nz), bf16),
-            pltpu.SemaphoreType.DMA((2,)),
-        ],
+        [pltpu.VMEM((8, 128), f32)],
         one // 4,
-    )(out, channel_rows, *map(in_hbm, pieces[1:]))
+    )(out, *pieces)
     cot_p = shift(cot, C, 1)
     (dpre_t,) = call(back_kernel, [VMEM] * 3, [((half, tokens), bf16)], (), one)(
         cot, out_mine, slope
@@ -557,7 +559,6 @@
     (joint,) = call(
         joint_kernel, [VMEM] * 10, [((nz, share, channels + width + 384), bf16)], (), one // 8
     )(last_own, last_small, *last, first_own, first_small, *first)
-    dpre_r, joint = lax.optimization_barrier((dpre_r, joint))
     joint = lax.all_to_all(joint, Z, split_axis=0, concat_axis=0, tiled=True)
     (grad_hidden,) = call(
         hidden_kernel,

time: 135 us -> 131 us (0.970)
  starting transfers between devices: 48.6 us -> 37.5 us
  waiting for transfers between devices: 43.5 us -> 53.4 us
  local copies, waits for them, and re-layouts: 3.01 us -> 0.01 us
    ppermute x23, starting transfers between devices: 43.7 us -> 32.6 us  [shift(): return lax.ppermute(x, axis, [(i, (i + k) % n) for i in range(n)])]
    ppermute x23, waiting for transfers between devices: 38.3 us -> 49 us  [shift(): return lax.ppermute(x, axis, [(i, (i + k) % n) for i in range(n)])]
    unnamed x20 -> x4, local copies, waits for them, and re-layouts: 1.95 us -> 0.01 us
  transfers between devices with their start and end apart: 24 -> 24, of which waited for: 16 -> 14; matrix products, arithmetic and copies ran while one was open for 1% -> 0% of each run, Pallas kernels for 17% -> 18%
where the time goes in v3:
time: 131 us; the launch traced here: 129 us
  waiting for transfers between devices  53.4 us (41%)
  Pallas kernels  37.8 us (29%)
  starting transfers between devices  37.5 us (29%)
    ppermute x23, waiting for transfers between devices, shift(): return lax.ppermute(x, axis, [(i, (i + k) % n) for i in range(n)])  49 us
    ppermute x23, starting transfers between devices, shift(): return lax.ppermute(x, axis, [(i, (i + k) % n) for i in range(n)])  32.6 us
    pallas_call x1, Pallas kernels, on_device(): call(first_kernel, [HBM, VMEM, HBM, HBM, HBM], [((half, tokens), bf16)] *...  7.89 us
    pallas_call x1, Pallas kernels, on_device(): call(hidden_kernel, [VMEM, VMEM, HBM], [((tokens, width), bf16)], [pltpu....  7.05 us
    pallas_call x1, Pallas kernels, on_device(): call(grad_in_kernel, [VMEM] * 6, messages(quarter, width)[1:] + [((ROWS,...  5.08 us
    all_to_all x1, starting transfers between devices, on_device(): joint = lax.all_to_all(joint, Z, split_axis=0, concat_axis=0, tiled=True)  4.88 us
    all_to_all x1, waiting for transfers between devices, on_device(): joint = lax.all_to_all(joint, Z, split_axis=0, concat_axis=0, tiled=True)  4.45 us
  transfers between devices with their start and end apart: 24, of which 14 were waited for; matrix products, arithmetic and copies ran while one was open for 0% of the time, Pallas kernels for 18%

profile of v3, /device:TPU:6, one launch (start us, length us, event | category | flops | bytes accessed | tf_op | source)
XLA Modules:
  0.0 129.5 jit_solution(12441346415696552968)
XLA Ops:
  0.7 3.0 %collective-permute-done.rows_p = bf16[512,1152]{1,0:T(8,128)(2,1)S(1)} collective-permute-done((bf16[512,1152]{1,0:T(8,128)(2,1)}, bf16[512,1152]{1,0:T(8,128)(2,1)S(1)}, u32[]{:S(2)}, u32[]{:S(2)}) %collective-permute-start) | collective-permute-done | bytes 1179680 | tf_op jit(solution)/shard_map/ppermute | solution.py:30
  3.8 7.9 %shard_map.109 = (bf16[1024,512]{1,0:T(8,128)(2,1)S(1)}, bf16[1024,512]{1,0:T(8,128)(2,1)S(1)}, f32[1024,512]{1,0:T(8,128)S(1)}, f32[1024,512]{1,0:T(8,128)S(1)}...) custom-call(bf16[512,1152]{1,0:T(8,128)(2,1)} %bitcast.11, ...), custom_call_target="tpu_custom_call" | custom-call | flops 2147483648 | bytes 4194304 | tf_op jit(solution)/shard_map/pallas_call | solution.py:466
  15.3 3.3 %collective-permute-start.3 = (bf16[512,128]{1,0:T(8,128)(2,1)S(1)}, bf16[512,128]{1,0:T(8,128)(2,1)S(1)}, u32[]{:S(2)}, u32[]{:S(2)}) collective-permute-start(bf16[512,128]{1,0:T(8,128)(2,1)S(1)} %get-tuple-element.58), channel_id=1, source_target_pairs={{0,2},{1,3},{2,4},{3,5},{4,6},{5,7},{6,0},{7,1},{8,10},{9,11},{10,... | collective-permute-start | bytes 393224 | tf_op jit(solution)/shard_map/ppermute | solution.py:30
  18.5 4.0 %collective-permute-start.4 = (bf16[512,128]{1,0:T(8,128)(2,1)S(1)}, bf16[512,128]{1,0:T(8,128)(2,1)S(1)}, u32[]{:S(2)}, u32[]{:S(2)}) collective-permute-start(bf16[512,128]{1,0:T(8,128)(2,1)S(1)} %get-tuple-element.59), channel_id=1, source_target_pairs={{0,3},{1,4},{2,5},{3,6},{4,7},{5,0},{6,1},{7,2},{8,11},{9,12},{10,... | collective-permute-start | bytes 393224 | tf_op jit(solution)/shard_map/ppermute | solution.py:30
  23.5 4.5 %collective-permute-start.6 = (bf16[512,128]{1,0:T(8,128)(2,1)S(1)}, bf16[512,128]{1,0:T(8,128)(2,1)S(1)}, u32[]{:S(2)}, u32[]{:S(2)}) collective-permute-start(bf16[512,128]{1,0:T(8,128)(2,1)S(1)} %get-tuple-element.61), channel_id=1, source_target_pairs={{0,5},{1,6},{2,7},{3,0},{4,1},{5,2},{6,3},{7,4},{8,13},{9,14},{10,... | collective-permute-start | bytes 393224 | tf_op jit(solution)/shard_map/ppermute | solution.py:30
  28.1 3.4 %collective-permute-done.3.refs_2_ = bf16[512,128]{1,0:T(8,128)(2,1)S(1)} collective-permute-done((bf16[512,128]{1,0:T(8,128)(2,1)S(1)}, bf16[512,128]{1,0:T(8,128)(2,1)S(1)}, u32[]{:S(2)}, u32[]{:S(2)}) %collective-permute-start.3) | collective-permute-done | bytes 131104 | tf_op jit(solution)/shard_map/ppermute | solution.py:30
  37.1 3.4 %collective-permute-done.4.refs_3_ = bf16[512,128]{1,0:T(8,128)(2,1)S(1)} collective-permute-done((bf16[512,128]{1,0:T(8,128)(2,1)S(1)}, bf16[512,128]{1,0:T(8,128)(2,1)S(1)}, u32[]{:S(2)}, u32[]{:S(2)}) %collective-permute-start.4) | collective-permute-done | bytes 131104 | tf_op jit(solution)/shard_map/ppermute | solution.py:30
  40.5 3.0 %collective-permute-done.6.refs_5_ = bf16[512,128]{1,0:T(8,128)(2,1)S(1)} collective-permute-done((bf16[512,128]{1,0:T(8,128)(2,1)S(1)}, bf16[512,128]{1,0:T(8,128)(2,1)S(1)}, u32[]{:S(2)}, u32[]{:S(2)}) %collective-permute-start.6) | collective-permute-done | bytes 131104 | tf_op jit(solution)/shard_map/ppermute | solution.py:30
  43.6 3.8 %collective-permute-done.7.refs_6_ = bf16[512,128]{1,0:T(8,128)(2,1)S(1)} collective-permute-done((bf16[512,128]{1,0:T(8,128)(2,1)S(1)}, bf16[512,128]{1,0:T(8,128)(2,1)S(1)}, u32[]{:S(2)}, u32[]{:S(2)}) %collective-permute-start.7) | collective-permute-done | bytes 131104 | tf_op jit(solution)/shard_map/ppermute | solution.py:30
  48.2 2.4 %shard_map.113.cot = bf16[520,1024]{1,0:T(8,128)(2,1)S(1)} custom-call(f32[512,1024]{1,0:T(8,128)S(1)} %shard_map.111.out, bf16[512,128]{1,0:T(8,128)(2,1)S(1)} %get-tuple-element.56.refs_0_, bf16[512,128]{1,0:T(8,128)(2,1)S(1)} %collective-permute-done.2.refs_1_, bf16[512,128]{1,0:T(8,128)(2,1)S(1)} %collective-permute-done.3.refs_2_, ...), custom_call_target="tpu_custom_call" | custom-call | flops 268435456 | bytes 4194304 | tf_op jit(solution)/shard_map/pallas_call | solution.py:491
  50.7 2.7 %collective-permute-done.9.cot_p = bf16[520,1024]{1,0:T(8,128)(2,1)S(1)} collective-permute-done((bf16[520,1024]{1,0:T(8,128)(2,1)S(1)}, bf16[520,1024]{1,0:T(8,128)(2,1)S(1)}, u32[]{:S(2)}, u32[]{:S(2)}) %collective-permute-start.9) | collective-permute-done | bytes 1064992 | tf_op jit(solution)/shard_map/ppermute | solution.py:30
  55.0 2.3 %shard_map.115 = (bf16[264,1024]{1,0:T(8,128)(2,1)S(1)}, bf16[264,1024]{1,0:T(8,128)(2,1)S(1)}, f32[256,1024]{1,0:T(8,128)S(1)}) custom-call(bf16[1024,512]{1,0:T(8,128)(2,1)S(1)} %get-tuple-element.50.act, bf16[1024,512]{1,0:T(8,128)(2,1)S(1)} %get-tuple-element.51.act_p, bf16[520,1024]{1,0:T(8,128)(2,1)S(1)} %shard_map.113.cot, ...), custom_call_target="tpu_custom_call" | custom-call | flops 2147483648 | bytes 4194304 | tf_op jit(solution)/shard_map/pallas_call | solution.py:532
  58.3 2.4 %collective-permute-start.12 = (bf16[264,1024]{1,0:T(8,128)(2,1)S(1)}, bf16[264,1024]{1,0:T(8,128)(2,1)S(1)}, u32[]{:S(2)}, u32[]{:S(2)}) collective-permute-start(bf16[264,1024]{1,0:T(8,128)(2,1)S(1)} %get-tuple-element.69), channel_id=1, source_target_pairs={{0,16},{16,32},{32,48},{48,0},{1,17},{17,33},{33,49},{49,1},{2,18}... | collective-permute-start | bytes 1622024 | tf_op jit(solution)/shard_map/ppermute | solution.py:30
  64.3 3.3 %collective-permute-start.16 = (bf16[264,1152]{1,0:T(8,128)(2,1)S(1)}, bf16[264,1152]{1,0:T(8,128)(2,1)S(1)}, u32[]{:S(2)}, u32[]{:S(2)}) collective-permute-start(bf16[264,1152]{1,0:T(8,128)(2,1)S(1)} %shard_map.119), channel_id=1, source_target_pairs={{0,128},{64,192},{128,0},{192,64},{1,129},{65,193},{129,1},{193,65... | collective-permute-start | bytes 1824776 | tf_op jit(solution)/shard_map/ppermute | solution.py:30
  67.8 5.1 %shard_map.118 = (bf16[264,1152]{1,0:T(8,128)(2,1)S(1)}, bf16[264,1152]{1,0:T(8,128)(2,1)S(1)}, f32[256,1152]{1,0:T(8,128)S(1)}, f32[8,128]{1,0:T(8,128)S(1)}, bf16[1024,512]{1,0:T(8,128)(2,1)S(1)}) custom-call(bf16[520,1024]{1,0:T(8,128)(2,1)S(1)} %collective-permute-done.9.cot_p, bf16[1024,1024]{1,0:T(8,128)(2,1)S(1)} %get-tuple-element.55.w.w_mine, ...), custom_call_target="tpu_custom_call" | custom-call | flops 3221225472 | bytes 4194304 | tf_op jit(solution)/shard_map/pallas_call | solution.py:515
  74.1 10.5 %collective-permute-done.11.g_b = bf16[264,1024]{1,0:T(8,128)(2,1)S(1)} collective-permute-done((bf16[264,1024]{1,0:T(8,128)(2,1)S(1)}, bf16[264,1024]{1,0:T(8,128)(2,1)S(1)}, u32[]{:S(2)}, u32[]{:S(2)}) %collective-permute-start.11) | collective-permute-done | bytes 540704 | tf_op jit(solution)/shard_map/ppermute | solution.py:30
  87.3 3.0 %collective-permute-start.13 = (bf16[72,1024]{1,0:T(8,128)(2,1)S(1)}, bf16[72,1024]{1,0:T(8,128)(2,1)S(1)}, u32[]{:S(2)}, u32[]{:S(2)}) collective-permute-start(bf16[72,1024]{1,0:T(8,128)(2,1)S(1)} %get-tuple-element.72), channel_id=1, source_target_pairs={{0,128},{64,192},{128,0},{192,64},{1,129},{65,193},{129,1},{193,65... | collective-permute-start | bytes 442376 | tf_op jit(solution)/shard_map/ppermute | solution.py:30
  91.7 4.2 %collective-permute-done.17.g_b = bf16[264,1152]{1,0:T(8,128)(2,1)S(1)} collective-permute-done((bf16[264,1152]{1,0:T(8,128)(2,1)S(1)}, bf16[264,1152]{1,0:T(8,128)(2,1)S(1)}, u32[]{:S(2)}, u32[]{:S(2)}) %collective-permute-start.17) | collective-permute-done | bytes 608288 | tf_op jit(solution)/shard_map/ppermute | solution.py:30
  95.9 5.4 %collective-permute-done.18.g_c = bf16[264,1152]{1,0:T(8,128)(2,1)S(1)} collective-permute-done((bf16[264,1152]{1,0:T(8,128)(2,1)S(1)}, bf16[264,1152]{1,0:T(8,128)(2,1)S(1)}, u32[]{:S(2)}, u32[]{:S(2)}) %collective-permute-start.18) | collective-permute-done | bytes 608288 | tf_op jit(solution)/shard_map/ppermute | solution.py:30
  102.1 3.1 %collective-permute-done.13.o2 = bf16[72,1024]{1,0:T(8,128)(2,1)S(1)} collective-permute-done((bf16[72,1024]{1,0:T(8,128)(2,1)S(1)}, bf16[72,1024]{1,0:T(8,128)(2,1)S(1)}, u32[]{:S(2)}, u32[]{:S(2)}) %collective-permute-start.13) | collective-permute-done | bytes 147488 | tf_op jit(solution)/shard_map/ppermute | solution.py:30
  106.4 5.1 %collective-permute-done.15.o3 = bf16[72,1024]{1,0:T(8,128)(2,1)S(1)} collective-permute-done((bf16[72,1024]{1,0:T(8,128)(2,1)S(1)}, bf16[72,1024]{1,0:T(8,128)(2,1)S(1)}, u32[]{:S(2)}, u32[]{:S(2)}) %collective-permute-start.15) | collective-permute-done | bytes 147488 | tf_op jit(solution)/shard_map/ppermute | solution.py:30
  112.4 4.9 %all-to-all-start = ((bf16[8,8,2560]{2,1,0:T(8,128)(2,1)}), bf16[8,8,2560]{2,1,0:T(8,128)(2,1)S(1)}, u32[]{:S(2)}, u32[]{:S(2)}) async-start(bf16[8,8,2560]{2,1,0:T(8,128)(2,1)} %shard_map.121), calls=%async_computation | async-start | bytes 655360 | tf_op jit(solution)/shard_map/all_to_all | solution.py:562
  117.3 7.1 %shard_map.124 = bf16[512,1152]{1,0:T(8,128)(2,1)} custom-call(bf16[512,1024]{1,0:T(8,128)(2,1)S(1)} %get-tuple-element.91.dpre, bf16[512,1024]{1,0:T(8,128)(2,1)S(1)} %collective-permute-done.22.dpre_r, bf16[4,4,2,64,1152]{4,3,2,1,0:T(8,128)(2,1)} %bitcast.16), custom_call_target="tpu_custom_call" | custom-call | flops 2147483648 | bytes 4194304 | tf_op jit(solution)/shard_map/pallas_call | solution.py:563
  124.4 4.5 %all-to-all-done.joint = bf16[8,8,2560]{2,1,0:T(8,128)(2,1)S(1)} async-done(((bf16[8,8,2560]{2,1,0:T(8,128)(2,1)}), bf16[8,8,2560]{2,1,0:T(8,128)(2,1)S(1)}, u32[]{:S(2)}, u32[]{:S(2)}) %all-to-all-start) | async-done | bytes 327712 | tf_op jit(solution)/shard_map/all_to_all | solution.py:562
  (44 shorter events, 26.3 us)
Async XLA Ops:
  0.6 3.1 %collective-permute-start = (bf16[512,1152]{1,0:T(8,128)(2,1)}, bf16[512,1152]{1,0:T(8,128)(2,1)S(1)}, u32[]{:S(2)}, u32[]{:S(2)}) collective-permute-start(bf16[512,1152]{1,0:T(8,128)(2,1)} %bitcast.10), channel_id=1, source_target_pairs={{0,8},{8,0},{1,9},{9,1},{2,10},{10,2},{3,11},{11,3},{4,12},{12,4},... | collective-permute-start | bytes 3538952 | tf_op jit(solution)/shard_map/ppermute | solution.py:30
  11.7 19.8 %collective-permute-start.1 = (bf16[512,1024]{1,0:T(8,128)(2,1)S(1)}, bf16[512,1024]{1,0:T(8,128)(2,1)S(1)}, u32[]{:S(2)}, u32[]{:S(2)}) collective-permute-start(bf16[512,1024]{1,0:T(8,128)(2,1)S(1)} %get-tuple-element.52), channel_id=1, source_target_pairs={{0,8},{8,0},{1,9},{9,1},{2,10},{10,2},{3,11},{11,3},{4,12},{12,4},... | collective-permute-start | bytes 3145736 | tf_op jit(solution)/shard_map/ppermute | solution.py:30
  13.3 10.3 %collective-permute-start.2 = (bf16[512,128]{1,0:T(8,128)(2,1)S(1)}, bf16[512,128]{1,0:T(8,128)(2,1)S(1)}, u32[]{:S(2)}, u32[]{:S(2)}) collective-permute-start(bf16[512,128]{1,0:T(8,128)(2,1)S(1)} %get-tuple-element.57), channel_id=1, source_target_pairs={{0,1},{1,2},{2,3},{3,4},{4,5},{5,6},{6,7},{7,0},{8,9},{9,10},{10,1... | collective-permute-start | bytes 393224 | tf_op jit(solution)/shard_map/ppermute | solution.py:30
  15.3 16.2 %collective-permute-start.3 = (bf16[512,128]{1,0:T(8,128)(2,1)S(1)}, bf16[512,128]{1,0:T(8,128)(2,1)S(1)}, u32[]{:S(2)}, u32[]{:S(2)}) collective-permute-start(bf16[512,128]{1,0:T(8,128)(2,1)S(1)} %get-tuple-element.58), channel_id=1, source_target_pairs={{0,2},{1,3},{2,4},{3,5},{4,6},{5,7},{6,0},{7,1},{8,10},{9,11},{10,... | collective-permute-start | bytes 393224 | tf_op jit(solution)/shard_map/ppermute | solution.py:30
  18.5 22.0 %collective-permute-start.4 = (bf16[512,128]{1,0:T(8,128)(2,1)S(1)}, bf16[512,128]{1,0:T(8,128)(2,1)S(1)}, u32[]{:S(2)}, u32[]{:S(2)}) collective-permute-start(bf16[512,128]{1,0:T(8,128)(2,1)S(1)} %get-tuple-element.59), channel_id=1, source_target_pairs={{0,3},{1,4},{2,5},{3,6},{4,7},{5,0},{6,1},{7,2},{8,11},{9,12},{10,... | collective-permute-start | bytes 393224 | tf_op jit(solution)/shard_map/ppermute | solution.py:30
  22.6 18.0 %collective-permute-start.5 = (bf16[512,128]{1,0:T(8,128)(2,1)S(1)}, bf16[512,128]{1,0:T(8,128)(2,1)S(1)}, u32[]{:S(2)}, u32[]{:S(2)}) collective-permute-start(bf16[512,128]{1,0:T(8,128)(2,1)S(1)} %get-tuple-element.60), channel_id=1, source_target_pairs={{0,4},{1,5},{2,6},{3,7},{4,0},{5,1},{6,2},{7,3},{8,12},{9,13},{10,... | collective-permute-start | bytes 393224 | tf_op jit(solution)/shard_map/ppermute | solution.py:30
  23.5 20.0 %collective-permute-start.6 = (bf16[512,128]{1,0:T(8,128)(2,1)S(1)}, bf16[512,128]{1,0:T(8,128)(2,1)S(1)}, u32[]{:S(2)}, u32[]{:S(2)}) collective-permute-start(bf16[512,128]{1,0:T(8,128)(2,1)S(1)} %get-tuple-element.61), channel_id=1, source_target_pairs={{0,5},{1,6},{2,7},{3,0},{4,1},{5,2},{6,3},{7,4},{8,13},{9,14},{10,... | collective-permute-start | bytes 393224 | tf_op jit(solution)/shard_map/ppermute | solution.py:30
  31.5 15.9 %collective-permute-start.7 = (bf16[512,128]{1,0:T(8,128)(2,1)S(1)}, bf16[512,128]{1,0:T(8,128)(2,1)S(1)}, u32[]{:S(2)}, u32[]{:S(2)}) collective-permute-start(bf16[512,128]{1,0:T(8,128)(2,1)S(1)} %get-tuple-element.62), channel_id=1, source_target_pairs={{0,6},{1,7},{2,0},{3,1},{4,2},{5,3},{6,4},{7,5},{8,14},{9,15},{10,... | collective-permute-start | bytes 393224 | tf_op jit(solution)/shard_map/ppermute | solution.py:30
  31.5 16.7 %collective-permute-start.8 = (bf16[512,128]{1,0:T(8,128)(2,1)S(1)}, bf16[512,128]{1,0:T(8,128)(2,1)S(1)}, u32[]{:S(2)}, u32[]{:S(2)}) collective-permute-start(bf16[512,128]{1,0:T(8,128)(2,1)S(1)} %get-tuple-element.63), channel_id=1, source_target_pairs={{0,7},{1,0},{2,1},{3,2},{4,3},{5,4},{6,5},{7,6},{8,15},{9,8},{10,9... | collective-permute-start | bytes 393224 | tf_op jit(solution)/shard_map/ppermute | solution.py:30
  50.6 2.8 %collective-permute-start.9 = (bf16[520,1024]{1,0:T(8,128)(2,1)S(1)}, bf16[520,1024]{1,0:T(8,128)(2,1)S(1)}, u32[]{:S(2)}, u32[]{:S(2)}) collective-permute-start(bf16[520,1024]{1,0:T(8,128)(2,1)S(1)} %shard_map.113.cot), channel_id=1, source_target_pairs={{0,8},{8,0},{1,9},{9,1},{2,10},{10,2},{3,11},{11,3},{4,12},{12,4},... | collective-permute-start | bytes 3194888 | tf_op jit(solution)/shard_map/ppermute | solution.py:30
  57.4 27.2 %collective-permute-start.11 = (bf16[264,1024]{1,0:T(8,128)(2,1)S(1)}, bf16[264,1024]{1,0:T(8,128)(2,1)S(1)}, u32[]{:S(2)}, u32[]{:S(2)}) collective-permute-start(bf16[264,1024]{1,0:T(8,128)(2,1)S(1)} %get-tuple-element.68), channel_id=1, source_target_pairs={{0,48},{16,0},{32,16},{48,32},{1,49},{17,1},{33,17},{49,33},{2,50}... | collective-permute-start | bytes 1622024 | tf_op jit(solution)/shard_map/ppermute | solution.py:30
  58.3 28.6 %collective-permute-start.12 = (bf16[264,1024]{1,0:T(8,128)(2,1)S(1)}, bf16[264,1024]{1,0:T(8,128)(2,1)S(1)}, u32[]{:S(2)}, u32[]{:S(2)}) collective-permute-start(bf16[264,1024]{1,0:T(8,128)(2,1)S(1)} %get-tuple-element.69), channel_id=1, source_target_pairs={{0,16},{16,32},{32,48},{48,0},{1,17},{17,33},{33,49},{49,1},{2,18}... | collective-permute-start | bytes 1622024 | tf_op jit(solution)/shard_map/ppermute | solution.py:30
  64.3 26.1 %collective-permute-start.16 = (bf16[264,1152]{1,0:T(8,128)(2,1)S(1)}, bf16[264,1152]{1,0:T(8,128)(2,1)S(1)}, u32[]{:S(2)}, u32[]{:S(2)}) collective-permute-start(bf16[264,1152]{1,0:T(8,128)(2,1)S(1)} %shard_map.119), channel_id=1, source_target_pairs={{0,128},{64,192},{128,0},{192,64},{1,129},{65,193},{129,1},{193,65... | collective-permute-start | bytes 1824776 | tf_op jit(solution)/shard_map/ppermute | solution.py:30
  67.6 19.5 %collective-permute-start.10 = (bf16[264,1024]{1,0:T(8,128)(2,1)S(1)}, bf16[264,1024]{1,0:T(8,128)(2,1)S(1)}, u32[]{:S(2)}, u32[]{:S(2)}) collective-permute-start(bf16[264,1024]{1,0:T(8,128)(2,1)S(1)} %get-tuple-element.67), channel_id=1, source_target_pairs={{0,32},{16,48},{32,0},{48,16},{1,33},{17,49},{33,1},{49,17},{2,34}... | collective-permute-start | bytes 1622024 | tf_op jit(solution)/shard_map/ppermute | solution.py:30
  72.9 23.0 %collective-permute-start.17 = (bf16[264,1152]{1,0:T(8,128)(2,1)S(1)}, bf16[264,1152]{1,0:T(8,128)(2,1)S(1)}, u32[]{:S(2)}, u32[]{:S(2)}) collective-permute-start(bf16[264,1152]{1,0:T(8,128)(2,1)S(1)} %get-tuple-element.79), channel_id=1, source_target_pairs={{0,192},{64,0},{128,64},{192,128},{1,193},{65,1},{129,65},{193,129... | collective-permute-start | bytes 1824776 | tf_op jit(solution)/shard_map/ppermute | solution.py:30
  84.6 16.8 %collective-permute-start.18 = (bf16[264,1152]{1,0:T(8,128)(2,1)S(1)}, bf16[264,1152]{1,0:T(8,128)(2,1)S(1)}, u32[]{:S(2)}, u32[]{:S(2)}) collective-permute-start(bf16[264,1152]{1,0:T(8,128)(2,1)S(1)} %get-tuple-element.80), channel_id=1, source_target_pairs={{0,64},{64,128},{128,192},{192,0},{1,65},{65,129},{129,193},{193,1... | collective-permute-start | bytes 1824776 | tf_op jit(solution)/shard_map/ppermute | solution.py:30
  87.0 30.4 %collective-permute-start.22 = (bf16[512,1024]{1,0:T(8,128)(2,1)S(1)}, bf16[512,1024]{1,0:T(8,128)(2,1)S(1)}, u32[]{:S(2)}, u32[]{:S(2)}) collective-permute-start(bf16[512,1024]{1,0:T(8,128)(2,1)S(1)} %get-tuple-element.92), channel_id=1, source_target_pairs={{0,8},{8,0},{1,9},{9,1},{2,10},{10,2},{3,11},{11,3},{4,12},{12,4},... | collective-permute-start | bytes 3145736 | tf_op jit(solution)/shard_map/ppermute | solution.py:30
  87.3 17.9 %collective-permute-start.13 = (bf16[72,1024]{1,0:T(8,128)(2,1)S(1)}, bf16[72,1024]{1,0:T(8,128)(2,1)S(1)}, u32[]{:S(2)}, u32[]{:S(2)}) collective-permute-start(bf16[72,1024]{1,0:T(8,128)(2,1)S(1)} %get-tuple-element.72), channel_id=1, source_target_pairs={{0,128},{64,192},{128,0},{192,64},{1,129},{65,193},{129,1},{193,65... | collective-permute-start | bytes 442376 | tf_op jit(solution)/shard_map/ppermute | solution.py:30
  90.3 14.8 %collective-permute-start.14 = (bf16[72,1024]{1,0:T(8,128)(2,1)S(1)}, bf16[72,1024]{1,0:T(8,128)(2,1)S(1)}, u32[]{:S(2)}, u32[]{:S(2)}) collective-permute-start(bf16[72,1024]{1,0:T(8,128)(2,1)S(1)} %get-tuple-element.73), channel_id=1, source_target_pairs={{0,192},{64,0},{128,64},{192,128},{1,193},{65,1},{129,65},{193,129... | collective-permute-start | bytes 442376 | tf_op jit(solution)/shard_map/ppermute | solution.py:30
  101.6 9.9 %collective-permute-start.19 = (bf16[72,1152]{1,0:T(8,128)(2,1)S(1)}, bf16[72,1152]{1,0:T(8,128)(2,1)S(1)}, u32[]{:S(2)}, u32[]{:S(2)}) collective-permute-start(bf16[72,1152]{1,0:T(8,128)(2,1)S(1)} %get-tuple-element.83), channel_id=1, source_target_pairs={{0,32},{16,48},{32,0},{48,16},{1,33},{17,49},{33,1},{49,17},{2,34}... | collective-permute-start | bytes 497672 | tf_op jit(solution)/shard_map/ppermute | solution.py:30
  101.7 9.8 %collective-permute-start.20 = (bf16[72,1152]{1,0:T(8,128)(2,1)S(1)}, bf16[72,1152]{1,0:T(8,128)(2,1)S(1)}, u32[]{:S(2)}, u32[]{:S(2)}) collective-permute-start(bf16[72,1152]{1,0:T(8,128)(2,1)S(1)} %get-tuple-element.84), channel_id=1, source_target_pairs={{0,48},{16,0},{32,16},{48,32},{1,49},{17,1},{33,17},{49,33},{2,50}... | collective-permute-start | bytes 497672 | tf_op jit(solution)/shard_map/ppermute | solution.py:30
  105.2 6.4 %collective-permute-start.21 = (bf16[72,1152]{1,0:T(8,128)(2,1)S(1)}, bf16[72,1152]{1,0:T(8,128)(2,1)S(1)}, u32[]{:S(2)}, u32[]{:S(2)}) collective-permute-start(bf16[72,1152]{1,0:T(8,128)(2,1)S(1)} %get-tuple-element.85), channel_id=1, source_target_pairs={{0,16},{16,32},{32,48},{48,0},{1,17},{17,33},{33,49},{49,1},{2,18}... | collective-permute-start | bytes 497672 | tf_op jit(solution)/shard_map/ppermute | solution.py:30
  105.2 6.4 %collective-permute-start.15 = (bf16[72,1024]{1,0:T(8,128)(2,1)S(1)}, bf16[72,1024]{1,0:T(8,128)(2,1)S(1)}, u32[]{:S(2)}, u32[]{:S(2)}) collective-permute-start(bf16[72,1024]{1,0:T(8,128)(2,1)S(1)} %get-tuple-element.74), channel_id=1, source_target_pairs={{0,64},{64,128},{128,192},{192,0},{1,65},{65,129},{129,193},{193,1... | collective-permute-start | bytes 442376 | tf_op jit(solution)/shard_map/ppermute | solution.py:30
  112.4 16.4 %all-to-all-start = ((bf16[8,8,2560]{2,1,0:T(8,128)(2,1)}), bf16[8,8,2560]{2,1,0:T(8,128)(2,1)S(1)}, u32[]{:S(2)}, u32[]{:S(2)}) async-start(bf16[8,8,2560]{2,1,0:T(8,128)(2,1)} %shard_map.121), calls=%async_computation | async-start | bytes 655360 | tf_op jit(solution)/shard_map/all_to_all | solution.py:562
  (2 other events, 31.3 us)
